TPU v7x, 32 devices: a whole 2x2x4 slice. The times are simulated.
32 devices in a mesh: dom: 32 (over z, y, x, core).
Axes of the slice: x: 2, y: 2, z: 4, core: 2. Of those that a mesh axis runs over, the one named last changes fastest.
Arguments:
- start_point: float32 [16384, 128], P('dom'), may hold values from -6 to 6
- residual: float32 [16384, 128], P('dom'), may hold values from -40 to 40
- direction: float32 [16384, 128], P('dom'), may hold values from -40 to 40
- send_list: int32 [32, 4, 3], P('dom'), may hold values from 0 to 3, as said below
- block_cols: int32 [128, 6], P('dom'), may hold values from 0 to 15, as said below
- block_vals: float32 [128, 6, 128, 128], P('dom'), may hold values from -0.2 to 8.1, as said below
Outputs:
- new_point: float32 [16384, 128], P('dom')
- new_residual: float32 [16384, 128], P('dom')
- new_direction: float32 [16384, 128], P('dom')
Inputs may be any that keep to these rules, and one draw needn't show every extreme that they name: send_list[t, m] lists, in its first entries, the distinct blocks of partition t that the partition at offset -off (off as in the first step) reads; between 1 and 3 of them are read for each pair, and some pair reads 3; the other entries are valid block numbers that are never read. `block_cols`: entry 0 of a block row names the row's own block; a block that couples two partitions appears in both partitions' rows, transposed; the assembled matrix is symmetric positive definite. `block_vals`: stored blocks that no coupling uses are zero.
All inputs are finite; a program needn't handle non-finite values.
Results may differ from a plain program's by a relative error of at most 0.0003.
Values sent between devices are 32-bit elements; how exact they have to be, the bound alone decides.
No kernel may reach another device: no remote copies, remote signals or barrier semaphores. Data moves between devices by JAX's collectives and lax.ppermute only.
A program may use at most 128 MiB of HBM per device.

v0:
```python
import jax
import jax.numpy as jnp
from jax import lax
from jax.sharding import PartitionSpec as P

STEPS = 6
BASIS = 13
center_value = 4.5
half_range = 4.5


def from_behind(shard, axis, by):
    peers = lax.axis_size(axis)
    return lax.ppermute(shard, axis, [(i, (i + by) % peers) for i in range(peers)])


def apply_blocks(blocked, send_rows, block_cols, block_vals):
    block_count, block_rows, width = blocked.shape
    highest = lax.Precision.HIGHEST
    flat_rows = blocked.reshape(block_count, block_rows * width)
    hop_count = send_rows.shape[0] // 2
    own_ids = jnp.arange(block_count, dtype=jnp.int32)
    pieces = [flat_rows]
    for slot_index in range(2 * hop_count):
        offset = slot_index + 1 if slot_index < hop_count else hop_count - 1 - slot_index
        chooser = (send_rows[slot_index][:, None] == own_ids[None, :]).astype(jnp.float32)
        outgoing = jnp.dot(chooser, flat_rows, precision=highest)
        pieces.append(from_behind(outgoing, "dom", -offset))
    ghost_table = jnp.concatenate(pieces, axis=0)
    ghost_ids = jnp.arange(ghost_table.shape[0], dtype=jnp.int32)
    running = jnp.zeros((block_count, block_rows, width), jnp.float32)
    for slot_index in range(block_cols.shape[1]):
        chooser = (block_cols[:, slot_index][:, None] == ghost_ids[None, :]).astype(jnp.float32)
        picked = jnp.dot(chooser, ghost_table, precision=highest).reshape(
            block_count, block_rows, width
        )
        running = running + jnp.einsum(
            "icb,ibw->icw", block_vals[:, slot_index], picked, precision=highest
        )
    return running


def next_vector(vector, send_rows, block_cols, block_vals):
    block_count = block_vals.shape[0]
    block_rows = block_vals.shape[2]
    blocked = vector.reshape(block_count, block_rows, vector.shape[1])
    image_part = apply_blocks(blocked, send_rows, block_cols, block_vals).reshape(vector.shape)
    return (image_part - center_value * vector) / half_range


def basis_change():
    positions = jnp.arange(BASIS)
    row_ids = positions[:, None]
    col_ids = positions[None, :]
    active = (col_ids < STEPS) | (col_ids > STEPS) & (col_ids < BASIS - 1)
    change_table = jnp.where(active & (row_ids == col_ids), center_value, 0.0)
    change_table = change_table + jnp.where(active & (row_ids == col_ids + 1), half_range, 0.0)
    return change_table.astype(jnp.float32)


def coefficient_steps(gram_matrix):
    change_table = basis_change()
    column_count = gram_matrix.shape[0]
    positions = jnp.arange(BASIS)
    point_c = jnp.zeros((column_count, BASIS), jnp.float32)
    resid_c = jnp.broadcast_to((positions == STEPS + 1).astype(jnp.float32), (column_count, BASIS))
    direc_c = jnp.broadcast_to((positions == 0).astype(jnp.float32), (column_count, BASIS))
    highest = lax.Precision.HIGHEST
    for step_index in range(STEPS):
        current = jnp.sum(
            resid_c * jnp.einsum("nab,nb->na", gram_matrix, resid_c, precision=highest), axis=1
        )
        moved_dir = jnp.einsum("ab,nb->na", change_table, direc_c, precision=highest)
        curvature = jnp.sum(
            direc_c * jnp.einsum("nab,nb->na", gram_matrix, moved_dir, precision=highest), axis=1
        )
        alpha_step = current / curvature
        point_c = point_c + alpha_step[:, None] * direc_c
        resid_c = resid_c - alpha_step[:, None] * moved_dir
        following = jnp.sum(
            resid_c * jnp.einsum("nab,nb->na", gram_matrix, resid_c, precision=highest), axis=1
        )
        direc_c = resid_c + (following / current)[:, None] * direc_c
    return (point_c, resid_c, direc_c)


def shards(start_point, residual, direction, send_list, block_cols, block_vals):
    send_rows = send_list[0]
    p_basis = [direction]
    r_basis = [residual]
    for power_step in range(STEPS):
        p_basis.append(next_vector(p_basis[-1], send_rows, block_cols, block_vals))
    for power_step in range(STEPS - 1):
        r_basis.append(next_vector(r_basis[-1], send_rows, block_cols, block_vals))
    basis_stack = jnp.stack(p_basis + r_basis)
    local_gram = jnp.einsum(
        "arn,brn->nab", basis_stack, basis_stack, precision=lax.Precision.HIGHEST
    )
    gram_matrix = lax.psum(local_gram, "dom")
    point_c, resid_c, direc_c = coefficient_steps(gram_matrix)
    highest = lax.Precision.HIGHEST
    new_point = start_point + jnp.einsum("na,arn->rn", point_c, basis_stack, precision=highest)
    new_residual = jnp.einsum("na,arn->rn", resid_c, basis_stack, precision=highest)
    new_direction = jnp.einsum("na,arn->rn", direc_c, basis_stack, precision=highest)
    return (new_point, new_residual, new_direction)


def solution(mesh):
    return jax.shard_map(
        shards,
        mesh=mesh,
        in_specs=(
            P("dom", None),
            P("dom", None),
            P("dom", None),
            P("dom", None, None),
            P("dom", None),
            P("dom", None, None, None),
        ),
        out_specs=(P("dom", None), P("dom", None), P("dom", None)),
        check_vma=False,
    )
```

profile of v0, /device:TPU:0, one launch (start us, length us, event | category | flops | bytes accessed | tf_op | source)
XLA Modules:
  0.0 516.2 jit_solution(13102410080200635533)
XLA Ops:
  7.2 1.2 slice_reduce_fusion.6
  9.9 6.5 %collective-permute-start.24 = (f32[3,16384]{1,0:T(4,128)S(1)}, f32[3,16384]{1,0:T(4,128)S(1)}, u32[]{:S(2)}, u32[]{:S(2)}) collective-permute-start(f32[3,16384]{1,0:T(4,128)S(1)} %fusion.361), channel_id=1, source_target_pairs={{0,31},{1,0},{2,1},{3,2},{4,3},{5,4},{6,5},{7,6},{8,7},{9,8},{10,9... | collective-permute-start | bytes 589832 | tf_op jit(solution)/shard_map/ppermute | solution.py:14
  18.6 1.3 collective-permute-start.27
  21.1 5.0 collective-permute-start
  32.6 7.7 %collective-permute-start.3 = (f32[3,16384]{1,0:T(4,128)}, f32[3,16384]{1,0:T(4,128)}, u32[]{:S(2)}, u32[]{:S(2)}) collective-permute-start(f32[3,16384]{1,0:T(4,128)} %fusion.334), channel_id=1, source_target_pairs={{0,2},{1,3},{2,4},{3,5},{4,6},{5,7},{6,8},{7,9},{8,10},{9,11},{10,... | collective-permute-start | bytes 589832 | tf_op jit(solution)/shard_map/ppermute | solution.py:14
  40.3 2.2 concatenate.39
  48.8 1.1 fusion.360
  53.3 6.4 %concatenate.33 = f32[16,16384]{1,0:T(8,128)S(1)} concatenate(f32[4,16384]{1,0:T(4,128)S(1)} %reshape_reshape.33, f32[3,16384]{1,0:T(4,128)} %collective-permute-done, f32[3,16384]{1,0:T(4,128)} %collective-permute-done.1, f32[3,16384]{1,0:T(4,128)} %collective-permute-done.2, f32[3,16384]{1,0:T(4,128)} %collective-permute-done.3), dimensions={0} | concatenate | bytes 2097152 | tf_op jit(solution)/shard_map/concatenate | solution.py:29
  69.0 2.6 collective-permute-start.28
  71.7 1.9 collective-permute-start.31
  73.6 5.0 collective-permute-start.4
  80.6 1.1 fusion.333
  81.7 1.9 collective-permute-start.5
  83.7 12.6 %collective-permute-start.7 = (f32[3,16384]{1,0:T(4,128)}, f32[3,16384]{1,0:T(4,128)}, u32[]{:S(2)}, u32[]{:S(2)}) collective-permute-start(f32[3,16384]{1,0:T(4,128)} %fusion.333), channel_id=1, source_target_pairs={{0,2},{1,3},{2,4},{3,5},{4,6},{5,7},{6,8},{7,9},{8,10},{9,11},{10,... | collective-permute-start | bytes 589832 | tf_op jit(solution)/shard_map/ppermute | solution.py:14
  96.2 6.5 %concatenate.40 = f32[16,16384]{1,0:T(8,128)S(1)} concatenate(f32[4,16384]{1,0:T(4,128)S(1)} %reshape_reshape.40, f32[3,16384]{1,0:T(4,128)} %copy-done.37, f32[3,16384]{1,0:T(4,128)} %copy-done.40, f32[3,16384]{1,0:T(4,128)} %copy-done.43, f32[3,16384]{1,0:T(4,128)} %collective-permute-done.31), dimensions={0} | concatenate | bytes 2097152 | tf_op jit(solution)/shard_map/concatenate | solution.py:29
  109.3 1.1 fusion.348
  113.2 6.7 %concatenate.34 = f32[16,16384]{1,0:T(8,128)S(1)} concatenate(f32[4,16384]{1,0:T(4,128)S(1)} %reshape_reshape.34, f32[3,16384]{1,0:T(4,128)} %collective-permute-done.4, f32[3,16384]{1,0:T(4,128)} %collective-permute-done.5, f32[3,16384]{1,0:T(4,128)} %collective-permute-done.6, f32[3,16384]{1,0:T(4,128)} %collective-permute-done.7), dimensions={0} | concatenate | bytes 2097152 | tf_op jit(solution)/shard_map/concatenate | solution.py:29
  126.4 1.1 fusion.343
  130.8 1.7 collective-permute-start.34
  132.9 4.6 collective-permute-start.32
  137.5 1.2 fusion.365
  139.3 1.5 collective-permute-done.34
  140.8 10.1 %collective-permute-start.9 = (f32[3,16384]{1,0:T(4,128)}, f32[3,16384]{1,0:T(4,128)}, u32[]{:S(2)}, u32[]{:S(2)}) collective-permute-start(f32[3,16384]{1,0:T(4,128)} %fusion.354), channel_id=1, source_target_pairs={{0,30},{1,31},{2,0},{3,1},{4,2},{5,3},{6,4},{7,5},{8,6},{9,7},{10,... | collective-permute-start | bytes 589832 | tf_op jit(solution)/shard_map/ppermute | solution.py:14
  151.0 5.4 %collective-permute-start.8 = (f32[3,16384]{1,0:T(4,128)}, f32[3,16384]{1,0:T(4,128)}, u32[]{:S(2)}, u32[]{:S(2)}) collective-permute-start(f32[3,16384]{1,0:T(4,128)} %fusion.365), channel_id=1, source_target_pairs={{0,31},{1,0},{2,1},{3,2},{4,3},{5,4},{6,5},{7,6},{8,7},{9,8},{10,9... | collective-permute-start | bytes 589832 | tf_op jit(solution)/shard_map/ppermute | solution.py:14
  156.4 3.3 concatenate.41
  166.3 1.1 fusion.358
  170.9 6.4 %concatenate.35 = f32[16,16384]{1,0:T(8,128)S(1)} concatenate(f32[4,16384]{1,0:T(4,128)S(1)} %reshape_reshape.35, f32[3,16384]{1,0:T(4,128)} %collective-permute-done.8, f32[3,16384]{1,0:T(4,128)} %collective-permute-done.9, f32[3,16384]{1,0:T(4,128)} %collective-permute-done.10, f32[3,16384]{1,0:T(4,128)} %collective-permute-done.11), dimensions={0} | concatenate | bytes 2097152 | tf_op jit(solution)/shard_map/concatenate | solution.py:29
  183.9 1.1 fusion.364
  188.2 3.5 collective-permute-start.38
  191.7 2.6 collective-permute-start.39
  195.3 4.1 collective-permute-start.12
  200.4 1.1 fusion.331
  201.6 4.5 collective-permute-done.37
  206.1 6.6 %collective-permute-start.15 = (f32[3,16384]{1,0:T(4,128)}, f32[3,16384]{1,0:T(4,128)}, u32[]{:S(2)}, u32[]{:S(2)}) collective-permute-start(f32[3,16384]{1,0:T(4,128)} %fusion.331), channel_id=1, source_target_pairs={{0,2},{1,3},{2,4},{3,5},{4,6},{5,7},{6,8},{7,9},{8,10},{9,11},{10,... | collective-permute-start | bytes 589832 | tf_op jit(solution)/shard_map/ppermute | solution.py:14
  212.7 6.5 %concatenate.42 = f32[16,16384]{1,0:T(8,128)S(1)} concatenate(f32[4,16384]{1,0:T(4,128)S(1)} %reshape_reshape.42, f32[3,16384]{1,0:T(4,128)} %copy-done.38, f32[3,16384]{1,0:T(4,128)} %copy-done.41, f32[3,16384]{1,0:T(4,128)} %copy-done.44, f32[3,16384]{1,0:T(4,128)} %collective-permute-done.39), dimensions={0} | concatenate | bytes 2097152 | tf_op jit(solution)/shard_map/concatenate | solution.py:29
  228.0 1.1 fusion.335
  229.1 1.1 fusion.324
  230.3 6.7 %concatenate.36 = f32[16,16384]{1,0:T(8,128)S(1)} concatenate(f32[4,16384]{1,0:T(4,128)S(1)} %reshape_reshape.36, f32[3,16384]{1,0:T(4,128)} %collective-permute-done.12, f32[3,16384]{1,0:T(4,128)} %collective-permute-done.13, f32[3,16384]{1,0:T(4,128)} %collective-permute-done.14, f32[3,16384]{1,0:T(4,128)} %collective-permute-done.15), dimensions={0} | concatenate | bytes 2097152 | tf_op jit(solution)/shard_map/concatenate | solution.py:29
  245.0 1.2 fusion.341
  246.2 2.7 collective-permute-start.40
  249.2 1.7 collective-permute-start.43
  251.9 5.1 collective-permute-start.16
  257.9 1.1 fusion.330
  259.1 1.4 collective-permute-start.17
  261.5 14.8 %collective-permute-start.19 = (f32[3,16384]{1,0:T(4,128)}, f32[3,16384]{1,0:T(4,128)}, u32[]{:S(2)}, u32[]{:S(2)}) collective-permute-start(f32[3,16384]{1,0:T(4,128)} %fusion.330), channel_id=1, source_target_pairs={{0,2},{1,3},{2,4},{3,5},{4,6},{5,7},{6,8},{7,9},{8,10},{9,11},{10,... | collective-permute-start | bytes 589832 | tf_op jit(solution)/shard_map/ppermute | solution.py:14
  276.4 6.2 %concatenate.43 = f32[16,16384]{1,0:T(8,128)S(1)} concatenate(f32[4,16384]{1,0:T(4,128)S(1)} %reshape_reshape.43, f32[3,16384]{1,0:T(4,128)} %copy-done.39, f32[3,16384]{1,0:T(4,128)} %copy-done.42, f32[3,16384]{1,0:T(4,128)} %copy-done.45, f32[3,16384]{1,0:T(4,128)} %collective-permute-done.43), dimensions={0} | concatenate | bytes 2097152 | tf_op jit(solution)/shard_map/concatenate | solution.py:29
  282.6 1.2 convolution_bitcast_fusion.5
  283.8 1.2 convolution_bitcast_fusion.4
  285.0 1.2 convolution_bitcast_fusion.3
  286.2 1.2 convolution_bitcast_fusion.2
  287.4 1.2 convolution_bitcast_fusion.1
  288.5 1.2 convolution_bitcast_fusion
  289.8 6.4 %concatenate.37 = f32[16,16384]{1,0:T(8,128)S(1)} concatenate(f32[4,16384]{1,0:T(4,128)S(1)} %reshape_reshape.37, f32[3,16384]{1,0:T(4,128)} %collective-permute-done.16, f32[3,16384]{1,0:T(4,128)} %collective-permute-done.17, f32[3,16384]{1,0:T(4,128)} %collective-permute-done.18, f32[3,16384]{1,0:T(4,128)} %collective-permute-done.19), dimensions={0} | concatenate | bytes 2097152 | tf_op jit(solution)/shard_map/concatenate | solution.py:29
  302.7 1.2 fusion.362
  308.4 2.7 collective-permute-start.20
  311.3 1.8 collective-permute-start.23
  314.7 3.0 collective-permute-done.20
  317.6 5.8 %collective-permute-done.21 = f32[3,16384]{1,0:T(4,128)S(1)} collective-permute-done((f32[3,16384]{1,0:T(4,128)}, f32[3,16384]{1,0:T(4,128)S(1)}, u32[]{:S(2)}, u32[]{:S(2)}) %collective-permute-start.21) | collective-permute-done | bytes 196640 | tf_op jit(solution)/shard_map/ppermute | solution.py:14
  324.8 6.2 %concatenate.38 = f32[16,16384]{1,0:T(8,128)S(1)} concatenate(f32[4,16384]{1,0:T(4,128)S(1)} %reshape_reshape.38, f32[3,16384]{1,0:T(4,128)} %copy-done.47, f32[3,16384]{1,0:T(4,128)} %copy-done.49, f32[3,16384]{1,0:T(4,128)} %copy-done.50, f32[3,16384]{1,0:T(4,128)} %collective-permute-done.23), dimensions={0} | concatenate | bytes 2097152 | tf_op jit(solution)/shard_map/concatenate | solution.py:29
  338.0 9.0 %stack.55 = f32[13,512,128]{1,0,2:T(8,128)} concatenate(f32[1,512,128]{1,0,2:T(1,128)S(1)} %copy-done.27, f32[1,512,128]{1,0,2:T(1,128)S(1)} %copy-done.30, f32[1,512,128]{1,0,2:T(1,128)S(1)} %copy-done.32, f32[1,512,128]{1,0,2:T(1,128)S(1)} %copy-done.34, f32[1,512,128]{1,0,2:T(1,128)S(1)} %copy-done.35, f32[1,512,128]{1,0,2:T(1,128)S(1)} %copy.74, f32[1,512,128]{1,0,2:T(1,128)S(1)} %copy.75, ...), dimensions={0} | concatenate | bytes 6815744 | tf_op jit(solution)/shard_map/stack | solution.py:95
  347.0 10.0 %fusion.499 = f32[128,13,13]{2,1,0:T(8,128)} fusion(f32[13,512,128]{1,0,2:T(8,128)} %stack.55), kind=kOutput, calls=%fused_computation.689 | convolution fusion | flops 132907008 | bytes 3494400 | tf_op jit(solution)/shard_map/arn,brn->nab/dot_general | solution.py:96
  357.2 134.9 %all-reduce.2.cloned.1.call-done = f32[128,13,13]{2,1,0:T(8,128)} async-done(((f32[128,13,13]{2,1,0:T(8,128)}), f32[128,13,13]{2,1,0:T(8,128)}) %all-reduce.2.cloned.1.call-update) | async-done | bytes 86544 | tf_op jit(solution)/shard_map/psum | solution.py:99
  492.1 1.9 multiply_reduce_fusion.14
  502.3 4.3 multiply_reduce_fusion
  (480 shorter events, 124.4 us)
Async XLA Ops:
  7.2 12.7 %copy-start.12 = (f32[512,128]{1,0:T(8,128)S(1)}, f32[512,128]{1,0:T(8,128)}, u32[]{:S(2)}) copy-start(f32[512,128]{1,0:T(8,128)} %param.8) | copy-start | bytes 786436
  7.2 484.9 %all-reduce.2.cloned.1.call-start = ((), (), s32[]{:S(2)}) async-start(), calls=%async_computation | async-start | bytes 2097152 | tf_op jit(solution)/shard_map/psum | solution.py:99
  9.5 16.6 %copy-start.13 = (f32[512,128]{1,0:T(8,128)S(1)}, f32[512,128]{1,0:T(8,128)}, u32[]{:S(2)}) copy-start(f32[512,128]{1,0:T(8,128)} %param.7) | copy-start | bytes 786436
  9.9 22.1 %collective-permute-start.24 = (f32[3,16384]{1,0:T(4,128)S(1)}, f32[3,16384]{1,0:T(4,128)S(1)}, u32[]{:S(2)}, u32[]{:S(2)}) collective-permute-start(f32[3,16384]{1,0:T(4,128)S(1)} %fusion.361), channel_id=1, source_target_pairs={{0,31},{1,0},{2,1},{3,2},{4,3},{5,4},{6,5},{7,6},{8,7},{9,8},{10,9... | collective-permute-start | bytes 589832 | tf_op jit(solution)/shard_map/ppermute | solution.py:14
  16.8 15.8 %collective-permute-start.25 = (f32[3,16384]{1,0:T(4,128)S(1)}, f32[3,16384]{1,0:T(4,128)S(1)}, u32[]{:S(2)}, u32[]{:S(2)}) collective-permute-start(f32[3,16384]{1,0:T(4,128)S(1)} %fusion.350), channel_id=1, source_target_pairs={{0,30},{1,31},{2,0},{3,1},{4,2},{5,3},{6,4},{7,5},{8,6},{9,7},{10,... | collective-permute-start | bytes 589832 | tf_op jit(solution)/shard_map/ppermute | solution.py:14
  17.9 14.7 %collective-permute-start.26 = (f32[3,16384]{1,0:T(4,128)S(1)}, f32[3,16384]{1,0:T(4,128)S(1)}, u32[]{:S(2)}, u32[]{:S(2)}) collective-permute-start(f32[3,16384]{1,0:T(4,128)S(1)} %fusion.339), channel_id=1, source_target_pairs={{0,1},{1,2},{2,3},{3,4},{4,5},{5,6},{6,7},{7,8},{8,9},{9,10},{10,1... | collective-permute-start | bytes 589832 | tf_op jit(solution)/shard_map/ppermute | solution.py:14
  18.6 21.8 %collective-permute-start.27 = (f32[3,16384]{1,0:T(4,128)S(1)}, f32[3,16384]{1,0:T(4,128)}, u32[]{:S(2)}, u32[]{:S(2)}) collective-permute-start(f32[3,16384]{1,0:T(4,128)S(1)} %fusion.328), channel_id=1, source_target_pairs={{0,2},{1,3},{2,4},{3,5},{4,6},{5,7},{6,8},{7,9},{8,10},{9,11},{10,... | collective-permute-start | bytes 589832 | tf_op jit(solution)/shard_map/ppermute | solution.py:14
  20.0 9.9 %copy-start.57 = (s32[4,6]{1,0:T(4,128)S(1)}, s32[4,6]{1,0:T(4,128)}, u32[]{:S(2)}) copy-start(s32[4,6]{1,0:T(4,128)} %param.10) | copy-start | bytes 292
  21.1 32.2 %collective-permute-start = (f32[3,16384]{1,0:T(4,128)}, f32[3,16384]{1,0:T(4,128)}, u32[]{:S(2)}, u32[]{:S(2)}) collective-permute-start(f32[3,16384]{1,0:T(4,128)} %fusion.367), channel_id=1, source_target_pairs={{0,31},{1,0},{2,1},{3,2},{4,3},{5,4},{6,5},{7,6},{8,7},{9,8},{10,9... | collective-permute-start | bytes 589832 | tf_op jit(solution)/shard_map/ppermute | solution.py:14
  26.3 22.2 %copy-start.4 = (f32[512,128]{0,1:T(8,128)}, f32[512,128]{0,1:T(8,128)S(1)}, u32[]{:S(2)}) copy-start(f32[512,128]{0,1:T(8,128)S(1)} %copy.60) | copy-start | bytes 786436
  29.8 35.4 %copy-start.2 = (f32[512,128]{0,1:T(8,128)}, f32[512,128]{0,1:T(8,128)S(1)}, u32[]{:S(2)}) copy-start(f32[512,128]{0,1:T(8,128)S(1)} %copy.47) | copy-start | bytes 786436
  32.0 21.3 %collective-permute-start.1 = (f32[3,16384]{1,0:T(4,128)}, f32[3,16384]{1,0:T(4,128)}, u32[]{:S(2)}, u32[]{:S(2)}) collective-permute-start(f32[3,16384]{1,0:T(4,128)} %fusion.356), channel_id=1, source_target_pairs={{0,30},{1,31},{2,0},{3,1},{4,2},{5,3},{6,4},{7,5},{8,6},{9,7},{10,... | collective-permute-start | bytes 589832 | tf_op jit(solution)/shard_map/ppermute | solution.py:14
  32.6 20.7 %collective-permute-start.2 = (f32[3,16384]{1,0:T(4,128)}, f32[3,16384]{1,0:T(4,128)}, u32[]{:S(2)}, u32[]{:S(2)}) collective-permute-start(f32[3,16384]{1,0:T(4,128)} %fusion.345), channel_id=1, source_target_pairs={{0,1},{1,2},{2,3},{3,4},{4,5},{5,6},{6,7},{7,8},{8,9},{9,10},{10,1... | collective-permute-start | bytes 589832 | tf_op jit(solution)/shard_map/ppermute | solution.py:14
  32.6 20.7 %collective-permute-start.3 = (f32[3,16384]{1,0:T(4,128)}, f32[3,16384]{1,0:T(4,128)}, u32[]{:S(2)}, u32[]{:S(2)}) collective-permute-start(f32[3,16384]{1,0:T(4,128)} %fusion.334), channel_id=1, source_target_pairs={{0,2},{1,3},{2,4},{3,5},{4,6},{5,7},{6,8},{7,9},{8,10},{9,11},{10,... | collective-permute-start | bytes 589832 | tf_op jit(solution)/shard_map/ppermute | solution.py:14
  65.2 6.5 %copy-start.51 = (f32[3,16384]{1,0:T(4,128)S(1)}, f32[3,16384]{1,0:T(4,128)}, u32[]{:S(2)}) copy-start(f32[3,16384]{1,0:T(4,128)} %fusion.327) | copy-start | bytes 589828
  65.3 13.4 %copy-start.11 = (f32[512,128]{0,1:T(8,128)S(1)}, f32[512,128]{0,1:T(8,128)}, u32[]{:S(2)}) copy-start(f32[512,128]{0,1:T(8,128)} %copy-done.10) | copy-start | bytes 786436
  69.0 12.8 %collective-permute-start.28 = (f32[3,16384]{1,0:T(4,128)S(1)}, f32[3,16384]{1,0:T(4,128)S(1)}, u32[]{:S(2)}, u32[]{:S(2)}) collective-permute-start(f32[3,16384]{1,0:T(4,128)S(1)} %copy-done.56), channel_id=1, source_target_pairs={{0,31},{1,0},{2,1},{3,2},{4,3},{5,4},{6,5},{7,6},{8,7},{9,8},{10,9... | collective-permute-start | bytes 589832 | tf_op jit(solution)/shard_map/ppermute | solution.py:14
  71.5 12.1 %collective-permute-start.29 = (f32[3,16384]{1,0:T(4,128)S(1)}, f32[3,16384]{1,0:T(4,128)S(1)}, u32[]{:S(2)}, u32[]{:S(2)}) collective-permute-start(f32[3,16384]{1,0:T(4,128)S(1)} %copy-done.55), channel_id=1, source_target_pairs={{0,30},{1,31},{2,0},{3,1},{4,2},{5,3},{6,4},{7,5},{8,6},{9,7},{10,... | collective-permute-start | bytes 589832 | tf_op jit(solution)/shard_map/ppermute | solution.py:14
  71.6 12.1 %collective-permute-start.30 = (f32[3,16384]{1,0:T(4,128)S(1)}, f32[3,16384]{1,0:T(4,128)S(1)}, u32[]{:S(2)}, u32[]{:S(2)}) collective-permute-start(f32[3,16384]{1,0:T(4,128)S(1)} %copy-done.53), channel_id=1, source_target_pairs={{0,1},{1,2},{2,3},{3,4},{4,5},{5,6},{6,7},{7,8},{8,9},{9,10},{10,1... | collective-permute-start | bytes 589832 | tf_op jit(solution)/shard_map/ppermute | solution.py:14
  71.7 24.5 %collective-permute-start.31 = (f32[3,16384]{1,0:T(4,128)S(1)}, f32[3,16384]{1,0:T(4,128)}, u32[]{:S(2)}, u32[]{:S(2)}) collective-permute-start(f32[3,16384]{1,0:T(4,128)S(1)} %copy-done.51), channel_id=1, source_target_pairs={{0,2},{1,3},{2,4},{3,5},{4,6},{5,7},{6,8},{7,9},{8,10},{9,11},{10,... | collective-permute-start | bytes 589832 | tf_op jit(solution)/shard_map/ppermute | solution.py:14
  73.6 39.5 %collective-permute-start.4 = (f32[3,16384]{1,0:T(4,128)}, f32[3,16384]{1,0:T(4,128)}, u32[]{:S(2)}, u32[]{:S(2)}) collective-permute-start(f32[3,16384]{1,0:T(4,128)} %fusion.366), channel_id=1, source_target_pairs={{0,31},{1,0},{2,1},{3,2},{4,3},{5,4},{6,5},{7,6},{8,7},{9,8},{10,9... | collective-permute-start | bytes 589832 | tf_op jit(solution)/shard_map/ppermute | solution.py:14
  81.7 14.5 %copy-start.37 = (f32[3,16384]{1,0:T(4,128)}, f32[3,16384]{1,0:T(4,128)S(1)}, u32[]{:S(2)}) copy-start(f32[3,16384]{1,0:T(4,128)S(1)} %collective-permute-done.28) | copy-start | bytes 589828
  81.7 31.4 %collective-permute-start.5 = (f32[3,16384]{1,0:T(4,128)}, f32[3,16384]{1,0:T(4,128)}, u32[]{:S(2)}, u32[]{:S(2)}) collective-permute-start(f32[3,16384]{1,0:T(4,128)} %fusion.355), channel_id=1, source_target_pairs={{0,30},{1,31},{2,0},{3,1},{4,2},{5,3},{6,4},{7,5},{8,6},{9,7},{10,... | collective-permute-start | bytes 589832 | tf_op jit(solution)/shard_map/ppermute | solution.py:14
  83.6 12.6 %copy-start.40 = (f32[3,16384]{1,0:T(4,128)}, f32[3,16384]{1,0:T(4,128)S(1)}, u32[]{:S(2)}) copy-start(f32[3,16384]{1,0:T(4,128)S(1)} %collective-permute-done.29) | copy-start | bytes 589828
  83.6 29.5 %collective-permute-start.6 = (f32[3,16384]{1,0:T(4,128)}, f32[3,16384]{1,0:T(4,128)}, u32[]{:S(2)}, u32[]{:S(2)}) collective-permute-start(f32[3,16384]{1,0:T(4,128)} %fusion.344), channel_id=1, source_target_pairs={{0,1},{1,2},{2,3},{3,4},{4,5},{5,6},{6,7},{7,8},{8,9},{9,10},{10,1... | collective-permute-start | bytes 589832 | tf_op jit(solution)/shard_map/ppermute | solution.py:14
  83.7 12.6 %copy-start.43 = (f32[3,16384]{1,0:T(4,128)}, f32[3,16384]{1,0:T(4,128)S(1)}, u32[]{:S(2)}) copy-start(f32[3,16384]{1,0:T(4,128)S(1)} %collective-permute-done.30) | copy-start | bytes 589828
  83.7 29.5 %collective-permute-start.7 = (f32[3,16384]{1,0:T(4,128)}, f32[3,16384]{1,0:T(4,128)}, u32[]{:S(2)}, u32[]{:S(2)}) collective-permute-start(f32[3,16384]{1,0:T(4,128)} %fusion.333), channel_id=1, source_target_pairs={{0,2},{1,3},{2,4},{3,5},{4,6},{5,7},{6,8},{7,9},{8,10},{9,11},{10,... | collective-permute-start | bytes 589832 | tf_op jit(solution)/shard_map/ppermute | solution.py:14
  129.8 9.1 %collective-permute-start.33 = (f32[3,16384]{1,0:T(4,128)}, f32[3,16384]{1,0:T(4,128)S(1)}, u32[]{:S(2)}, u32[]{:S(2)}) collective-permute-start(f32[3,16384]{1,0:T(4,128)} %fusion.348), channel_id=1, source_target_pairs={{0,30},{1,31},{2,0},{3,1},{4,2},{5,3},{6,4},{7,5},{8,6},{9,7},{10,... | collective-permute-start | bytes 589832 | tf_op jit(solution)/shard_map/ppermute | solution.py:14
  130.8 10.0 %collective-permute-start.34 = (f32[3,16384]{1,0:T(4,128)S(1)}, f32[3,16384]{1,0:T(4,128)S(1)}, u32[]{:S(2)}, u32[]{:S(2)}) collective-permute-start(f32[3,16384]{1,0:T(4,128)S(1)} %copy-done.54), channel_id=1, source_target_pairs={{0,1},{1,2},{2,3},{3,4},{4,5},{5,6},{6,7},{7,8},{8,9},{9,10},{10,1... | collective-permute-start | bytes 589832 | tf_op jit(solution)/shard_map/ppermute | solution.py:14
  132.5 18.5 %collective-permute-start.35 = (f32[3,16384]{1,0:T(4,128)S(1)}, f32[3,16384]{1,0:T(4,128)S(1)}, u32[]{:S(2)}, u32[]{:S(2)}) collective-permute-start(f32[3,16384]{1,0:T(4,128)S(1)} %copy-done.52), channel_id=1, source_target_pairs={{0,2},{1,3},{2,4},{3,5},{4,6},{5,7},{6,8},{7,9},{8,10},{9,11},{10,... | collective-permute-start | bytes 589832 | tf_op jit(solution)/shard_map/ppermute | solution.py:14
  132.9 23.6 %collective-permute-start.32 = (f32[3,16384]{1,0:T(4,128)S(1)}, f32[3,16384]{1,0:T(4,128)}, u32[]{:S(2)}, u32[]{:S(2)}) collective-permute-start(f32[3,16384]{1,0:T(4,128)S(1)} %fusion.359), channel_id=1, source_target_pairs={{0,31},{1,0},{2,1},{3,2},{4,3},{5,4},{6,5},{7,6},{8,7},{9,8},{10,9... | collective-permute-start | bytes 589832 | tf_op jit(solution)/shard_map/ppermute | solution.py:14
  137.5 33.3 %collective-permute-start.10 = (f32[3,16384]{1,0:T(4,128)}, f32[3,16384]{1,0:T(4,128)}, u32[]{:S(2)}, u32[]{:S(2)}) collective-permute-start(f32[3,16384]{1,0:T(4,128)} %fusion.343), channel_id=1, source_target_pairs={{0,1},{1,2},{2,3},{3,4},{4,5},{5,6},{6,7},{7,8},{8,9},{9,10},{10,1... | collective-permute-start | bytes 589832 | tf_op jit(solution)/shard_map/ppermute | solution.py:14
  138.9 32.0 %collective-permute-start.11 = (f32[3,16384]{1,0:T(4,128)}, f32[3,16384]{1,0:T(4,128)}, u32[]{:S(2)}, u32[]{:S(2)}) collective-permute-start(f32[3,16384]{1,0:T(4,128)} %fusion.332), channel_id=1, source_target_pairs={{0,2},{1,3},{2,4},{3,5},{4,6},{5,7},{6,8},{7,9},{8,10},{9,11},{10,... | collective-permute-start | bytes 589832 | tf_op jit(solution)/shard_map/ppermute | solution.py:14
  140.8 15.6 %copy-start.46 = (f32[3,16384]{1,0:T(4,128)}, f32[3,16384]{1,0:T(4,128)S(1)}, u32[]{:S(2)}) copy-start(f32[3,16384]{1,0:T(4,128)S(1)} %collective-permute-done.34) | copy-start | bytes 589828
  140.8 30.0 %collective-permute-start.9 = (f32[3,16384]{1,0:T(4,128)}, f32[3,16384]{1,0:T(4,128)}, u32[]{:S(2)}, u32[]{:S(2)}) collective-permute-start(f32[3,16384]{1,0:T(4,128)} %fusion.354), channel_id=1, source_target_pairs={{0,30},{1,31},{2,0},{3,1},{4,2},{5,3},{6,4},{7,5},{8,6},{9,7},{10,... | collective-permute-start | bytes 589832 | tf_op jit(solution)/shard_map/ppermute | solution.py:14
  151.0 19.9 %collective-permute-start.8 = (f32[3,16384]{1,0:T(4,128)}, f32[3,16384]{1,0:T(4,128)}, u32[]{:S(2)}, u32[]{:S(2)}) collective-permute-start(f32[3,16384]{1,0:T(4,128)} %fusion.365), channel_id=1, source_target_pairs={{0,31},{1,0},{2,1},{3,2},{4,3},{5,4},{6,5},{7,6},{8,7},{9,8},{10,9... | collective-permute-start | bytes 589832 | tf_op jit(solution)/shard_map/ppermute | solution.py:14
  183.6 10.7 %copy-start.18 = (f32[1,512,128]{1,2,0:T(8,128)S(1)}, f32[1,512,128]{1,2,0:T(8,128)}, u32[]{:S(2)}) copy-start(f32[1,512,128]{1,2,0:T(8,128)} %get-tuple-element.35) | copy-start | bytes 786436
  187.2 14.3 %collective-permute-start.36 = (f32[3,16384]{1,0:T(4,128)}, f32[3,16384]{1,0:T(4,128)S(1)}, u32[]{:S(2)}, u32[]{:S(2)}) collective-permute-start(f32[3,16384]{1,0:T(4,128)} %fusion.358), channel_id=1, source_target_pairs={{0,31},{1,0},{2,1},{3,2},{4,3},{5,4},{6,5},{7,6},{8,7},{9,8},{10,9... | collective-permute-start | bytes 589832 | tf_op jit(solution)/shard_map/ppermute | solution.py:14
  187.9 18.1 %collective-permute-start.37 = (f32[3,16384]{1,0:T(4,128)}, f32[3,16384]{1,0:T(4,128)S(1)}, u32[]{:S(2)}, u32[]{:S(2)}) collective-permute-start(f32[3,16384]{1,0:T(4,128)} %fusion.347), channel_id=1, source_target_pairs={{0,30},{1,31},{2,0},{3,1},{4,2},{5,3},{6,4},{7,5},{8,6},{9,7},{10,... | collective-permute-start | bytes 589832 | tf_op jit(solution)/shard_map/ppermute | solution.py:14
  188.2 17.9 %collective-permute-start.38 = (f32[3,16384]{1,0:T(4,128)}, f32[3,16384]{1,0:T(4,128)S(1)}, u32[]{:S(2)}, u32[]{:S(2)}) collective-permute-start(f32[3,16384]{1,0:T(4,128)} %fusion.336), channel_id=1, source_target_pairs={{0,1},{1,2},{2,3},{3,4},{4,5},{5,6},{6,7},{7,8},{8,9},{9,10},{10,1... | collective-permute-start | bytes 589832 | tf_op jit(solution)/shard_map/ppermute | solution.py:14
  191.7 20.9 %collective-permute-start.39 = (f32[3,16384]{1,0:T(4,128)}, f32[3,16384]{1,0:T(4,128)}, u32[]{:S(2)}, u32[]{:S(2)}) collective-permute-start(f32[3,16384]{1,0:T(4,128)} %fusion.325), channel_id=1, source_target_pairs={{0,2},{1,3},{2,4},{3,5},{4,6},{5,7},{6,8},{7,9},{8,10},{9,11},{10,... | collective-permute-start | bytes 589832 | tf_op jit(solution)/shard_map/ppermute | solution.py:14
  195.3 35.0 %collective-permute-start.12 = (f32[3,16384]{1,0:T(4,128)}, f32[3,16384]{1,0:T(4,128)}, u32[]{:S(2)}, u32[]{:S(2)}) collective-permute-start(f32[3,16384]{1,0:T(4,128)} %fusion.364), channel_id=1, source_target_pairs={{0,31},{1,0},{2,1},{3,2},{4,3},{5,4},{6,5},{7,6},{8,7},{9,8},{10,9... | collective-permute-start | bytes 589832 | tf_op jit(solution)/shard_map/ppermute | solution.py:14
  201.5 11.1 %copy-start.38 = (f32[3,16384]{1,0:T(4,128)}, f32[3,16384]{1,0:T(4,128)S(1)}, u32[]{:S(2)}) copy-start(f32[3,16384]{1,0:T(4,128)S(1)} %collective-permute-done.36) | copy-start | bytes 589828
  201.5 28.7 %collective-permute-start.13 = (f32[3,16384]{1,0:T(4,128)}, f32[3,16384]{1,0:T(4,128)}, u32[]{:S(2)}, u32[]{:S(2)}) collective-permute-start(f32[3,16384]{1,0:T(4,128)} %fusion.353), channel_id=1, source_target_pairs={{0,30},{1,31},{2,0},{3,1},{4,2},{5,3},{6,4},{7,5},{8,6},{9,7},{10,... | collective-permute-start | bytes 589832 | tf_op jit(solution)/shard_map/ppermute | solution.py:14
  206.1 6.6 %copy-start.41 = (f32[3,16384]{1,0:T(4,128)}, f32[3,16384]{1,0:T(4,128)S(1)}, u32[]{:S(2)}) copy-start(f32[3,16384]{1,0:T(4,128)S(1)} %collective-permute-done.37) | copy-start | bytes 589828
  206.1 24.2 %collective-permute-start.14 = (f32[3,16384]{1,0:T(4,128)}, f32[3,16384]{1,0:T(4,128)}, u32[]{:S(2)}, u32[]{:S(2)}) collective-permute-start(f32[3,16384]{1,0:T(4,128)} %fusion.342), channel_id=1, source_target_pairs={{0,1},{1,2},{2,3},{3,4},{4,5},{5,6},{6,7},{7,8},{8,9},{9,10},{10,1... | collective-permute-start | bytes 589832 | tf_op jit(solution)/shard_map/ppermute | solution.py:14
  206.1 6.6 %copy-start.44 = (f32[3,16384]{1,0:T(4,128)}, f32[3,16384]{1,0:T(4,128)S(1)}, u32[]{:S(2)}) copy-start(f32[3,16384]{1,0:T(4,128)S(1)} %collective-permute-done.38) | copy-start | bytes 589828
  206.1 24.2 %collective-permute-start.15 = (f32[3,16384]{1,0:T(4,128)}, f32[3,16384]{1,0:T(4,128)}, u32[]{:S(2)}, u32[]{:S(2)}) collective-permute-start(f32[3,16384]{1,0:T(4,128)} %fusion.331), channel_id=1, source_target_pairs={{0,2},{1,3},{2,4},{3,5},{4,6},{5,7},{6,8},{7,9},{8,10},{9,11},{10,... | collective-permute-start | bytes 589832 | tf_op jit(solution)/shard_map/ppermute | solution.py:14
  242.5 8.4 %copy-start.19 = (f32[1,512,128]{1,2,0:T(8,128)S(1)}, f32[1,512,128]{1,2,0:T(8,128)}, u32[]{:S(2)}) copy-start(f32[1,512,128]{1,2,0:T(8,128)} %get-tuple-element.34) | copy-start | bytes 786436
  246.2 12.9 %collective-permute-start.40 = (f32[3,16384]{1,0:T(4,128)}, f32[3,16384]{1,0:T(4,128)S(1)}, u32[]{:S(2)}, u32[]{:S(2)}) collective-permute-start(f32[3,16384]{1,0:T(4,128)} %fusion.357), channel_id=1, source_target_pairs={{0,31},{1,0},{2,1},{3,2},{4,3},{5,4},{6,5},{7,6},{8,7},{9,8},{10,9... | collective-permute-start | bytes 589832 | tf_op jit(solution)/shard_map/ppermute | solution.py:14
  248.9 12.6 %collective-permute-start.41 = (f32[3,16384]{1,0:T(4,128)}, f32[3,16384]{1,0:T(4,128)S(1)}, u32[]{:S(2)}, u32[]{:S(2)}) collective-permute-start(f32[3,16384]{1,0:T(4,128)} %fusion.346), channel_id=1, source_target_pairs={{0,30},{1,31},{2,0},{3,1},{4,2},{5,3},{6,4},{7,5},{8,6},{9,7},{10,... | collective-permute-start | bytes 589832 | tf_op jit(solution)/shard_map/ppermute | solution.py:14
  248.9 12.6 %collective-permute-start.42 = (f32[3,16384]{1,0:T(4,128)}, f32[3,16384]{1,0:T(4,128)S(1)}, u32[]{:S(2)}, u32[]{:S(2)}) collective-permute-start(f32[3,16384]{1,0:T(4,128)} %fusion.335), channel_id=1, source_target_pairs={{0,1},{1,2},{2,3},{3,4},{4,5},{5,6},{6,7},{7,8},{8,9},{9,10},{10,1... | collective-permute-start | bytes 589832 | tf_op jit(solution)/shard_map/ppermute | solution.py:14
  249.2 27.2 %collective-permute-start.43 = (f32[3,16384]{1,0:T(4,128)}, f32[3,16384]{1,0:T(4,128)}, u32[]{:S(2)}, u32[]{:S(2)}) collective-permute-start(f32[3,16384]{1,0:T(4,128)} %fusion.324), channel_id=1, source_target_pairs={{0,2},{1,3},{2,4},{3,5},{4,6},{5,7},{6,8},{7,9},{8,10},{9,11},{10,... | collective-permute-start | bytes 589832 | tf_op jit(solution)/shard_map/ppermute | solution.py:14
  251.9 37.8 %collective-permute-start.16 = (f32[3,16384]{1,0:T(4,128)}, f32[3,16384]{1,0:T(4,128)}, u32[]{:S(2)}, u32[]{:S(2)}) collective-permute-start(f32[3,16384]{1,0:T(4,128)} %fusion.363), channel_id=1, source_target_pairs={{0,31},{1,0},{2,1},{3,2},{4,3},{5,4},{6,5},{7,6},{8,7},{9,8},{10,9... | collective-permute-start | bytes 589832 | tf_op jit(solution)/shard_map/ppermute | solution.py:14
  259.1 17.3 %copy-start.39 = (f32[3,16384]{1,0:T(4,128)}, f32[3,16384]{1,0:T(4,128)S(1)}, u32[]{:S(2)}) copy-start(f32[3,16384]{1,0:T(4,128)S(1)} %collective-permute-done.40) | copy-start | bytes 589828
  259.1 30.7 %collective-permute-start.17 = (f32[3,16384]{1,0:T(4,128)}, f32[3,16384]{1,0:T(4,128)}, u32[]{:S(2)}, u32[]{:S(2)}) collective-permute-start(f32[3,16384]{1,0:T(4,128)} %fusion.352), channel_id=1, source_target_pairs={{0,30},{1,31},{2,0},{3,1},{4,2},{5,3},{6,4},{7,5},{8,6},{9,7},{10,... | collective-permute-start | bytes 589832 | tf_op jit(solution)/shard_map/ppermute | solution.py:14
  261.5 14.9 %copy-start.42 = (f32[3,16384]{1,0:T(4,128)}, f32[3,16384]{1,0:T(4,128)S(1)}, u32[]{:S(2)}) copy-start(f32[3,16384]{1,0:T(4,128)S(1)} %collective-permute-done.41) | copy-start | bytes 589828
  261.5 28.2 %collective-permute-start.18 = (f32[3,16384]{1,0:T(4,128)}, f32[3,16384]{1,0:T(4,128)}, u32[]{:S(2)}, u32[]{:S(2)}) collective-permute-start(f32[3,16384]{1,0:T(4,128)} %fusion.341), channel_id=1, source_target_pairs={{0,1},{1,2},{2,3},{3,4},{4,5},{5,6},{6,7},{7,8},{8,9},{9,10},{10,1... | collective-permute-start | bytes 589832 | tf_op jit(solution)/shard_map/ppermute | solution.py:14
  261.5 14.9 %copy-start.45 = (f32[3,16384]{1,0:T(4,128)}, f32[3,16384]{1,0:T(4,128)S(1)}, u32[]{:S(2)}) copy-start(f32[3,16384]{1,0:T(4,128)S(1)} %collective-permute-done.42) | copy-start | bytes 589828
  261.5 28.2 %collective-permute-start.19 = (f32[3,16384]{1,0:T(4,128)}, f32[3,16384]{1,0:T(4,128)}, u32[]{:S(2)}, u32[]{:S(2)}) collective-permute-start(f32[3,16384]{1,0:T(4,128)} %fusion.330), channel_id=1, source_target_pairs={{0,2},{1,3},{2,4},{3,5},{4,6},{5,7},{6,8},{7,9},{8,10},{9,11},{10,... | collective-permute-start | bytes 589832 | tf_op jit(solution)/shard_map/ppermute | solution.py:14
  308.4 9.2 %collective-permute-start.20 = (f32[3,16384]{1,0:T(4,128)}, f32[3,16384]{1,0:T(4,128)S(1)}, u32[]{:S(2)}, u32[]{:S(2)}) collective-permute-start(f32[3,16384]{1,0:T(4,128)} %fusion.362), channel_id=1, source_target_pairs={{0,31},{1,0},{2,1},{3,2},{4,3},{5,4},{6,5},{7,6},{8,7},{9,8},{10,9... | collective-permute-start | bytes 589832 | tf_op jit(solution)/shard_map/ppermute | solution.py:14
  311.1 12.3 %collective-permute-start.21 = (f32[3,16384]{1,0:T(4,128)}, f32[3,16384]{1,0:T(4,128)S(1)}, u32[]{:S(2)}, u32[]{:S(2)}) collective-permute-start(f32[3,16384]{1,0:T(4,128)} %fusion.351), channel_id=1, source_target_pairs={{0,30},{1,31},{2,0},{3,1},{4,2},{5,3},{6,4},{7,5},{8,6},{9,7},{10,... | collective-permute-start | bytes 589832 | tf_op jit(solution)/shard_map/ppermute | solution.py:14
  311.1 12.3 %collective-permute-start.22 = (f32[3,16384]{1,0:T(4,128)S(1)}, f32[3,16384]{1,0:T(4,128)S(1)}, u32[]{:S(2)}, u32[]{:S(2)}) collective-permute-start(f32[3,16384]{1,0:T(4,128)S(1)} %fusion.340), channel_id=1, source_target_pairs={{0,1},{1,2},{2,3},{3,4},{4,5},{5,6},{6,7},{7,8},{8,9},{9,10},{10,1... | collective-permute-start | bytes 589832 | tf_op jit(solution)/shard_map/ppermute | solution.py:14
  311.3 13.5 %collective-permute-start.23 = (f32[3,16384]{1,0:T(4,128)S(1)}, f32[3,16384]{1,0:T(4,128)}, u32[]{:S(2)}, u32[]{:S(2)}) collective-permute-start(f32[3,16384]{1,0:T(4,128)S(1)} %fusion.329), channel_id=1, source_target_pairs={{0,2},{1,3},{2,4},{3,5},{4,6},{5,7},{6,8},{7,9},{8,10},{9,11},{10,... | collective-permute-start | bytes 589832 | tf_op jit(solution)/shard_map/ppermute | solution.py:14
  (39 other events, 93.7 us)
Sparse Core Ops, SparseCore 0:
  357.2 134.8 all-reduce.1
where the time goes:
time: 523 us; the launch traced here: 516 us
  waiting for transfers between devices  151 us (29%)
  starting transfers between devices  119 us (23%)
  matrix products  117 us (22%)
  local copies, waits for them, and re-layouts  95.6 us (18%)
  other arithmetic  17 us (3%)
  between operations  16.7 us (3%)
    psum x1, waiting for transfers between devices, shards(): gram_matrix = lax.psum(local_gram, 'dom')  135 us
    ppermute x44, starting transfers between devices, from_behind(): lax.ppermute(shard, axis, [(i, (i + by) % peers) for i in range(peers)])  118 us
    concatenate x11, local copies, waits for them, and re-layouts, apply_blocks(): ghost_table = jnp.concatenate(pieces, axis=0)  63.5 us
    dot_general x44, matrix products, apply_blocks(): outgoing = jnp.dot(chooser, flat_rows, precision=highest)  44.7 us
    dot_general x66, matrix products, apply_blocks(): jnp.dot(chooser, ghost_table, precision=highest)  36.4 us
    dot_general x66, matrix products, apply_blocks(): jnp.einsum('icb,ibw->icw', block_vals[:, slot_index], picked, precision=h...  25.3 us
    another operation x14, local copies, waits for them, and re-layouts, shards(): basis_stack = jnp.stack(p_basis + r_basis)  18.5 us
    ppermute x44, waiting for transfers between devices, from_behind(): lax.ppermute(shard, axis, [(i, (i + by) % peers) for i in range(peers)])  16 us
  transfers between devices with their start and end apart: 45, of which 7 were waited for; matrix products, arithmetic and copies ran while one was open for 18% of the time, Pallas kernels for 0%

commit v1 on v0

--- a/solution.py
+++ b/solution.py
@@ -96,7 +96,7 @@
     local_gram = jnp.einsum(
         "arn,brn->nab", basis_stack, basis_stack, precision=lax.Precision.HIGHEST
     )
-    gram_matrix = lax.psum(local_gram, "dom")
+    gram_matrix = jnp.sum(jax.lax.all_gather(local_gram, axis_name="dom"), 0)
     point_c, resid_c, direc_c = coefficient_steps(gram_matrix)
     highest = lax.Precision.HIGHEST
     new_point = start_point + jnp.einsum("na,arn->rn", point_c, basis_stack, precision=highest)

time: 523 us -> 456 us (0.87)
  waiting for transfers between devices: 151 us -> 82.4 us
  local copies, waits for them, and re-layouts: 95.6 us -> 101 us
    psum x1 -> x0, waiting for transfers between devices: 135 us -> none  [shards(): gram_matrix = lax.psum(local_gram, 'dom')]
    all_gather x0 -> x1, waiting for transfers between devices: none -> 67.1 us  [shards(): gram_matrix = jnp.sum(jax.lax.all_gather(local_gram, axis_name='dom'), 0)]
    unnamed x13 -> x1, other arithmetic: 10.1 us -> 4.24 us
  transfers between devices with their start and end apart: 45 -> 45, of which waited for: 7 -> 8; matrix products, arithmetic and copies ran while one was open for 18% -> 21% of each run, Pallas kernels for 0% -> 0%
where the time goes in v1:
time: 456 us; the launch traced here: 449 us
  starting transfers between devices  118 us (26%)
  matrix products  117 us (26%)
  local copies, waits for them, and re-layouts  101 us (22%)
  waiting for transfers between devices  82.4 us (18%)
  between operations  16.5 us (4%)
  other arithmetic  13.1 us (3%)
    ppermute x44, starting transfers between devices, from_behind(): lax.ppermute(shard, axis, [(i, (i + by) % peers) for i in range(peers)])  118 us
    all_gather x1, waiting for transfers between devices, shards(): gram_matrix = jnp.sum(jax.lax.all_gather(local_gram, axis_name='dom'), 0)  67.1 us
    concatenate x11, local copies, waits for them, and re-layouts, apply_blocks(): ghost_table = jnp.concatenate(pieces, axis=0)  63.7 us
    dot_general x44, matrix products, apply_blocks(): outgoing = jnp.dot(chooser, flat_rows, precision=highest)  45.3 us
    dot_general x66, matrix products, apply_blocks(): jnp.dot(chooser, ghost_table, precision=highest)  36.4 us
    dot_general x66, matrix products, apply_blocks(): jnp.einsum('icb,ibw->icw', block_vals[:, slot_index], picked, precision=h...  25.3 us
    another operation x14, local copies, waits for them, and re-layouts, shards(): basis_stack = jnp.stack(p_basis + r_basis)  19 us
    ppermute x44, waiting for transfers between devices, from_behind(): lax.ppermute(shard, axis, [(i, (i + by) % peers) for i in range(peers)])  15.3 us
  transfers between devices with their start and end apart: 45, of which 8 were waited for; matrix products, arithmetic and copies ran while one was open for 21% of the time, Pallas kernels for 0%

profile of v1, /device:TPU:0, one launch (start us, length us, event | category | flops | bytes accessed | tf_op | source)
XLA Modules:
  0.0 448.7 jit_solution(2974008798314820287)
XLA Ops:
  7.2 1.2 slice_reduce_fusion.6
  9.9 6.5 %collective-permute-start.24 = (f32[3,16384]{1,0:T(4,128)S(1)}, f32[3,16384]{1,0:T(4,128)S(1)}, u32[]{:S(2)}, u32[]{:S(2)}) collective-permute-start(f32[3,16384]{1,0:T(4,128)S(1)} %fusion.361), channel_id=1, source_target_pairs={{0,31},{1,0},{2,1},{3,2},{4,3},{5,4},{6,5},{7,6},{8,7},{9,8},{10,9... | collective-permute-start | bytes 589832 | tf_op jit(solution)/shard_map/ppermute | solution.py:14
  18.6 1.3 collective-permute-start.27
  21.1 5.0 %collective-permute-start = (f32[3,16384]{1,0:T(4,128)}, f32[3,16384]{1,0:T(4,128)}, u32[]{:S(2)}, u32[]{:S(2)}) collective-permute-start(f32[3,16384]{1,0:T(4,128)} %fusion.367), channel_id=1, source_target_pairs={{0,31},{1,0},{2,1},{3,2},{4,3},{5,4},{6,5},{7,6},{8,7},{9,8},{10,9... | collective-permute-start | bytes 589832 | tf_op jit(solution)/shard_map/ppermute | solution.py:14
  27.4 1.1 fusion.345
  32.4 8.0 %collective-permute-start.3 = (f32[3,16384]{1,0:T(4,128)}, f32[3,16384]{1,0:T(4,128)}, u32[]{:S(2)}, u32[]{:S(2)}) collective-permute-start(f32[3,16384]{1,0:T(4,128)} %fusion.334), channel_id=1, source_target_pairs={{0,2},{1,3},{2,4},{3,5},{4,6},{5,7},{6,8},{7,9},{8,10},{9,11},{10,... | collective-permute-start | bytes 589832 | tf_op jit(solution)/shard_map/ppermute | solution.py:14
  40.3 2.2 concatenate.39
  49.4 1.1 fusion.360
  50.6 1.1 fusion.349
  54.0 6.4 %concatenate.33 = f32[16,16384]{1,0:T(8,128)S(1)} concatenate(f32[4,16384]{1,0:T(4,128)S(1)} %reshape_reshape.33, f32[3,16384]{1,0:T(4,128)} %collective-permute-done, f32[3,16384]{1,0:T(4,128)} %collective-permute-done.1, f32[3,16384]{1,0:T(4,128)} %collective-permute-done.2, f32[3,16384]{1,0:T(4,128)} %collective-permute-done.3), dimensions={0} | concatenate | bytes 2097152 | tf_op jit(solution)/shard_map/concatenate | solution.py:29
  70.2 2.6 collective-permute-start.28
  72.9 1.9 collective-permute-start.31
  74.8 5.1 %collective-permute-start.4 = (f32[3,16384]{1,0:T(4,128)}, f32[3,16384]{1,0:T(4,128)}, u32[]{:S(2)}, u32[]{:S(2)}) collective-permute-start(f32[3,16384]{1,0:T(4,128)} %fusion.366), channel_id=1, source_target_pairs={{0,31},{1,0},{2,1},{3,2},{4,3},{5,4},{6,5},{7,6},{8,7},{9,8},{10,9... | collective-permute-start | bytes 589832 | tf_op jit(solution)/shard_map/ppermute | solution.py:14
  82.9 1.9 collective-permute-start.5
  84.9 12.7 %collective-permute-start.7 = (f32[3,16384]{1,0:T(4,128)}, f32[3,16384]{1,0:T(4,128)}, u32[]{:S(2)}, u32[]{:S(2)}) collective-permute-start(f32[3,16384]{1,0:T(4,128)} %fusion.333), channel_id=1, source_target_pairs={{0,2},{1,3},{2,4},{3,5},{4,6},{5,7},{6,8},{7,9},{8,10},{9,11},{10,... | collective-permute-start | bytes 589832 | tf_op jit(solution)/shard_map/ppermute | solution.py:14
  97.7 6.5 %concatenate.40 = f32[16,16384]{1,0:T(8,128)S(1)} concatenate(f32[4,16384]{1,0:T(4,128)S(1)} %reshape_reshape.40, f32[3,16384]{1,0:T(4,128)} %copy-done.36, f32[3,16384]{1,0:T(4,128)} %copy-done.39, f32[3,16384]{1,0:T(4,128)} %copy-done.42, f32[3,16384]{1,0:T(4,128)} %collective-permute-done.31), dimensions={0} | concatenate | bytes 2097152 | tf_op jit(solution)/shard_map/concatenate | solution.py:29
  114.6 6.7 %concatenate.34 = f32[16,16384]{1,0:T(8,128)S(1)} concatenate(f32[4,16384]{1,0:T(4,128)S(1)} %reshape_reshape.34, f32[3,16384]{1,0:T(4,128)} %collective-permute-done.4, f32[3,16384]{1,0:T(4,128)} %collective-permute-done.5, f32[3,16384]{1,0:T(4,128)} %collective-permute-done.6, f32[3,16384]{1,0:T(4,128)} %collective-permute-done.7), dimensions={0} | concatenate | bytes 2097152 | tf_op jit(solution)/shard_map/concatenate | solution.py:29
  127.8 1.1 fusion.343
  132.3 1.8 collective-permute-start.34
  134.3 4.8 %collective-permute-start.32 = (f32[3,16384]{1,0:T(4,128)S(1)}, f32[3,16384]{1,0:T(4,128)}, u32[]{:S(2)}, u32[]{:S(2)}) collective-permute-start(f32[3,16384]{1,0:T(4,128)S(1)} %fusion.359), channel_id=1, source_target_pairs={{0,31},{1,0},{2,1},{3,2},{4,3},{5,4},{6,5},{7,6},{8,7},{9,8},{10,9... | collective-permute-start | bytes 589832 | tf_op jit(solution)/shard_map/ppermute | solution.py:14
  139.0 1.1 fusion.365
  140.8 1.4 collective-permute-done.34
  142.2 10.1 %collective-permute-start.9 = (f32[3,16384]{1,0:T(4,128)}, f32[3,16384]{1,0:T(4,128)}, u32[]{:S(2)}, u32[]{:S(2)}) collective-permute-start(f32[3,16384]{1,0:T(4,128)} %fusion.354), channel_id=1, source_target_pairs={{0,30},{1,31},{2,0},{3,1},{4,2},{5,3},{6,4},{7,5},{8,6},{9,7},{10,... | collective-permute-start | bytes 589832 | tf_op jit(solution)/shard_map/ppermute | solution.py:14
  152.3 5.4 %collective-permute-start.8 = (f32[3,16384]{1,0:T(4,128)}, f32[3,16384]{1,0:T(4,128)}, u32[]{:S(2)}, u32[]{:S(2)}) collective-permute-start(f32[3,16384]{1,0:T(4,128)} %fusion.365), channel_id=1, source_target_pairs={{0,31},{1,0},{2,1},{3,2},{4,3},{5,4},{6,5},{7,6},{8,7},{9,8},{10,9... | collective-permute-start | bytes 589832 | tf_op jit(solution)/shard_map/ppermute | solution.py:14
  157.8 3.3 concatenate.41
  167.7 1.1 fusion.358
  171.1 1.1 fusion.325
  172.2 6.4 %concatenate.35 = f32[16,16384]{1,0:T(8,128)S(1)} concatenate(f32[4,16384]{1,0:T(4,128)S(1)} %reshape_reshape.35, f32[3,16384]{1,0:T(4,128)} %collective-permute-done.8, f32[3,16384]{1,0:T(4,128)} %collective-permute-done.9, f32[3,16384]{1,0:T(4,128)} %collective-permute-done.10, f32[3,16384]{1,0:T(4,128)} %collective-permute-done.11), dimensions={0} | concatenate | bytes 2097152 | tf_op jit(solution)/shard_map/concatenate | solution.py:29
  185.2 1.1 fusion.364
  189.6 3.5 collective-permute-start.38
  193.1 2.6 collective-permute-start.39
  196.7 4.1 collective-permute-start.12
  203.0 4.5 collective-permute-done.37
  207.5 6.5 %collective-permute-start.15 = (f32[3,16384]{1,0:T(4,128)}, f32[3,16384]{1,0:T(4,128)}, u32[]{:S(2)}, u32[]{:S(2)}) collective-permute-start(f32[3,16384]{1,0:T(4,128)} %fusion.331), channel_id=1, source_target_pairs={{0,2},{1,3},{2,4},{3,5},{4,6},{5,7},{6,8},{7,9},{8,10},{9,11},{10,... | collective-permute-start | bytes 589832 | tf_op jit(solution)/shard_map/ppermute | solution.py:14
  214.0 6.5 %concatenate.42 = f32[16,16384]{1,0:T(8,128)S(1)} concatenate(f32[4,16384]{1,0:T(4,128)S(1)} %reshape_reshape.42, f32[3,16384]{1,0:T(4,128)} %copy-done.37, f32[3,16384]{1,0:T(4,128)} %copy-done.40, f32[3,16384]{1,0:T(4,128)} %copy-done.43, f32[3,16384]{1,0:T(4,128)} %collective-permute-done.39), dimensions={0} | concatenate | bytes 2097152 | tf_op jit(solution)/shard_map/concatenate | solution.py:29
  229.3 1.1 fusion.335
  231.6 6.7 %concatenate.36 = f32[16,16384]{1,0:T(8,128)S(1)} concatenate(f32[4,16384]{1,0:T(4,128)S(1)} %reshape_reshape.36, f32[3,16384]{1,0:T(4,128)} %collective-permute-done.12, f32[3,16384]{1,0:T(4,128)} %collective-permute-done.13, f32[3,16384]{1,0:T(4,128)} %collective-permute-done.14, f32[3,16384]{1,0:T(4,128)} %collective-permute-done.15), dimensions={0} | concatenate | bytes 2097152 | tf_op jit(solution)/shard_map/concatenate | solution.py:29
  246.4 1.1 fusion.341
  247.5 2.7 collective-permute-start.40
  250.6 1.6 collective-permute-start.43
  253.2 5.1 %collective-permute-start.16 = (f32[3,16384]{1,0:T(4,128)}, f32[3,16384]{1,0:T(4,128)}, u32[]{:S(2)}, u32[]{:S(2)}) collective-permute-start(f32[3,16384]{1,0:T(4,128)} %fusion.363), channel_id=1, source_target_pairs={{0,31},{1,0},{2,1},{3,2},{4,3},{5,4},{6,5},{7,6},{8,7},{9,8},{10,9... | collective-permute-start | bytes 589832 | tf_op jit(solution)/shard_map/ppermute | solution.py:14
  259.2 1.1 fusion.330
  260.4 1.5 collective-permute-start.17
  263.0 14.1 %collective-permute-start.19 = (f32[3,16384]{1,0:T(4,128)}, f32[3,16384]{1,0:T(4,128)}, u32[]{:S(2)}, u32[]{:S(2)}) collective-permute-start(f32[3,16384]{1,0:T(4,128)} %fusion.330), channel_id=1, source_target_pairs={{0,2},{1,3},{2,4},{3,5},{4,6},{5,7},{6,8},{7,9},{8,10},{9,11},{10,... | collective-permute-start | bytes 589832 | tf_op jit(solution)/shard_map/ppermute | solution.py:14
  277.1 6.2 %concatenate.43 = f32[16,16384]{1,0:T(8,128)S(1)} concatenate(f32[4,16384]{1,0:T(4,128)S(1)} %reshape_reshape.43, f32[3,16384]{1,0:T(4,128)} %copy-done.38, f32[3,16384]{1,0:T(4,128)} %copy-done.41, f32[3,16384]{1,0:T(4,128)} %copy-done.44, f32[3,16384]{1,0:T(4,128)} %collective-permute-done.43), dimensions={0} | concatenate | bytes 2097152 | tf_op jit(solution)/shard_map/concatenate | solution.py:29
  283.3 1.2 convolution_bitcast_fusion.5
  284.5 1.2 convolution_bitcast_fusion.4
  285.7 1.2 convolution_bitcast_fusion.3
  286.8 1.2 convolution_bitcast_fusion.2
  288.0 1.2 convolution_bitcast_fusion.1
  289.2 1.2 convolution_bitcast_fusion
  290.5 6.4 %concatenate.37 = f32[16,16384]{1,0:T(8,128)S(1)} concatenate(f32[4,16384]{1,0:T(4,128)S(1)} %reshape_reshape.37, f32[3,16384]{1,0:T(4,128)} %collective-permute-done.16, f32[3,16384]{1,0:T(4,128)} %collective-permute-done.17, f32[3,16384]{1,0:T(4,128)} %collective-permute-done.18, f32[3,16384]{1,0:T(4,128)} %collective-permute-done.19), dimensions={0} | concatenate | bytes 2097152 | tf_op jit(solution)/shard_map/concatenate | solution.py:29
  303.8 1.1 fusion.351
  309.1 2.7 collective-permute-start.20
  312.0 1.8 collective-permute-start.23
  316.0 2.3 collective-permute-done.20
  318.3 5.8 %collective-permute-done.21 = f32[3,16384]{1,0:T(4,128)S(1)} collective-permute-done((f32[3,16384]{1,0:T(4,128)}, f32[3,16384]{1,0:T(4,128)S(1)}, u32[]{:S(2)}, u32[]{:S(2)}) %collective-permute-start.21) | collective-permute-done | bytes 196640 | tf_op jit(solution)/shard_map/ppermute | solution.py:14
  325.5 6.4 %concatenate.38 = f32[16,16384]{1,0:T(8,128)S(1)} concatenate(f32[4,16384]{1,0:T(4,128)S(1)} %reshape_reshape.38, f32[3,16384]{1,0:T(4,128)} %copy-done.46, f32[3,16384]{1,0:T(4,128)} %copy-done.48, f32[3,16384]{1,0:T(4,128)} %copy-done.49, f32[3,16384]{1,0:T(4,128)} %collective-permute-done.23), dimensions={0} | concatenate | bytes 2097152 | tf_op jit(solution)/shard_map/concatenate | solution.py:29
  339.0 8.8 %stack.55 = f32[13,512,128]{1,0,2:T(8,128)} concatenate(f32[1,512,128]{1,0,2:T(1,128)S(1)} %copy-done.25, f32[1,512,128]{1,0,2:T(1,128)S(1)} %copy-done.28, f32[1,512,128]{1,0,2:T(1,128)S(1)} %copy-done.30, f32[1,512,128]{1,0,2:T(1,128)S(1)} %copy-done.32, f32[1,512,128]{1,0,2:T(1,128)S(1)} %copy-done.34, f32[1,512,128]{1,0,2:T(1,128)S(1)} %copy.155, f32[1,512,128]{1,0,2:T(1,128)S(1)} %copy.156, ...), dimensions={0} | concatenate | bytes 6815744 | tf_op jit(solution)/shard_map/stack | solution.py:95
  347.8 9.0 %fusion.499 = f32[128,13,13]{2,1,0:T(8,128)S(1)} fusion(f32[13,512,128]{1,0,2:T(8,128)} %stack.55), kind=kOutput, calls=%fused_computation.689 | convolution fusion | flops 132907008 | bytes 3494400 | tf_op jit(solution)/shard_map/arn,brn->nab/dot_general | solution.py:96
  358.1 67.1 %all-gather.3.cloned.1.call-done = f32[4096,13,13]{0,2,1:T(8,128)} async-done(((f32[128,13,13]{0,2,1:T(8,128)}), f32[4096,13,13]{0,2,1:T(8,128)}) %all-gather.3.cloned.1.call-update) | async-done | bytes 2768912 | tf_op jit(solution)/shard_map/all_gather | solution.py:99
  425.2 4.6 %reshape.408 = f32[32,128,13,13]{1,0,3,2:T(8,128)} reshape(f32[4096,13,13]{0,2,1:T(8,128)} %all-gather.3.cloned.1.call-done) | data formatting | bytes 5537792 | tf_op jit(solution)/shard_map/all_gather | solution.py:99
  429.8 2.2 reduce_sum.121
  434.7 4.2 multiply_reduce_fusion
  (451 shorter events, 123.2 us)
Async XLA Ops:
  7.2 12.7 %copy-start.11 = (f32[512,128]{1,0:T(8,128)S(1)}, f32[512,128]{1,0:T(8,128)}, u32[]{:S(2)}) copy-start(f32[512,128]{1,0:T(8,128)} %param.8) | copy-start | bytes 786436
  7.2 418.0 %all-gather.3.cloned.1.call-start = ((), (), s32[]{:S(2)}) async-start(), calls=%async_computation | async-start | bytes 3514368 | tf_op jit(solution)/shard_map/all_gather | solution.py:99
  9.5 16.6 %copy-start.12 = (f32[512,128]{1,0:T(8,128)S(1)}, f32[512,128]{1,0:T(8,128)}, u32[]{:S(2)}) copy-start(f32[512,128]{1,0:T(8,128)} %param.7) | copy-start | bytes 786436
  9.9 21.8 %collective-permute-start.24 = (f32[3,16384]{1,0:T(4,128)S(1)}, f32[3,16384]{1,0:T(4,128)S(1)}, u32[]{:S(2)}, u32[]{:S(2)}) collective-permute-start(f32[3,16384]{1,0:T(4,128)S(1)} %fusion.361), channel_id=1, source_target_pairs={{0,31},{1,0},{2,1},{3,2},{4,3},{5,4},{6,5},{7,6},{8,7},{9,8},{10,9... | collective-permute-start | bytes 589832 | tf_op jit(solution)/shard_map/ppermute | solution.py:14
  16.8 15.5 %collective-permute-start.25 = (f32[3,16384]{1,0:T(4,128)S(1)}, f32[3,16384]{1,0:T(4,128)S(1)}, u32[]{:S(2)}, u32[]{:S(2)}) collective-permute-start(f32[3,16384]{1,0:T(4,128)S(1)} %fusion.350), channel_id=1, source_target_pairs={{0,30},{1,31},{2,0},{3,1},{4,2},{5,3},{6,4},{7,5},{8,6},{9,7},{10,... | collective-permute-start | bytes 589832 | tf_op jit(solution)/shard_map/ppermute | solution.py:14
  17.9 14.5 %collective-permute-start.26 = (f32[3,16384]{1,0:T(4,128)S(1)}, f32[3,16384]{1,0:T(4,128)S(1)}, u32[]{:S(2)}, u32[]{:S(2)}) collective-permute-start(f32[3,16384]{1,0:T(4,128)S(1)} %fusion.339), channel_id=1, source_target_pairs={{0,1},{1,2},{2,3},{3,4},{4,5},{5,6},{6,7},{7,8},{8,9},{9,10},{10,1... | collective-permute-start | bytes 589832 | tf_op jit(solution)/shard_map/ppermute | solution.py:14
  18.5 10.1 %copy-start.53 = (s32[4,6]{1,0:T(4,128)S(1)}, s32[4,6]{1,0:T(4,128)}, u32[]{:S(2)}) copy-start(s32[4,6]{1,0:T(4,128)} %param.10) | copy-start | bytes 292
  18.6 21.8 %collective-permute-start.27 = (f32[3,16384]{1,0:T(4,128)S(1)}, f32[3,16384]{1,0:T(4,128)}, u32[]{:S(2)}, u32[]{:S(2)}) collective-permute-start(f32[3,16384]{1,0:T(4,128)S(1)} %fusion.328), channel_id=1, source_target_pairs={{0,2},{1,3},{2,4},{3,5},{4,6},{5,7},{6,8},{7,9},{8,10},{9,11},{10,... | collective-permute-start | bytes 589832 | tf_op jit(solution)/shard_map/ppermute | solution.py:14
  21.1 32.8 %collective-permute-start = (f32[3,16384]{1,0:T(4,128)}, f32[3,16384]{1,0:T(4,128)}, u32[]{:S(2)}, u32[]{:S(2)}) collective-permute-start(f32[3,16384]{1,0:T(4,128)} %fusion.367), channel_id=1, source_target_pairs={{0,31},{1,0},{2,1},{3,2},{4,3},{5,4},{6,5},{7,6},{8,7},{9,8},{10,9... | collective-permute-start | bytes 589832 | tf_op jit(solution)/shard_map/ppermute | solution.py:14
  26.3 22.2 %copy-start.3 = (f32[512,128]{0,1:T(8,128)}, f32[512,128]{0,1:T(8,128)S(1)}, u32[]{:S(2)}) copy-start(f32[512,128]{0,1:T(8,128)S(1)} %copy.141) | copy-start | bytes 786436
  28.7 37.2 %copy-start.1 = (f32[512,128]{0,1:T(8,128)}, f32[512,128]{0,1:T(8,128)S(1)}, u32[]{:S(2)}) copy-start(f32[512,128]{0,1:T(8,128)S(1)} %copy.128) | copy-start | bytes 786436
  31.8 22.2 %collective-permute-start.1 = (f32[3,16384]{1,0:T(4,128)}, f32[3,16384]{1,0:T(4,128)}, u32[]{:S(2)}, u32[]{:S(2)}) collective-permute-start(f32[3,16384]{1,0:T(4,128)} %fusion.356), channel_id=1, source_target_pairs={{0,30},{1,31},{2,0},{3,1},{4,2},{5,3},{6,4},{7,5},{8,6},{9,7},{10,... | collective-permute-start | bytes 589832 | tf_op jit(solution)/shard_map/ppermute | solution.py:14
  32.3 21.6 %collective-permute-start.2 = (f32[3,16384]{1,0:T(4,128)}, f32[3,16384]{1,0:T(4,128)}, u32[]{:S(2)}, u32[]{:S(2)}) collective-permute-start(f32[3,16384]{1,0:T(4,128)} %fusion.345), channel_id=1, source_target_pairs={{0,1},{1,2},{2,3},{3,4},{4,5},{5,6},{6,7},{7,8},{8,9},{9,10},{10,1... | collective-permute-start | bytes 589832 | tf_op jit(solution)/shard_map/ppermute | solution.py:14
  32.4 21.6 %collective-permute-start.3 = (f32[3,16384]{1,0:T(4,128)}, f32[3,16384]{1,0:T(4,128)}, u32[]{:S(2)}, u32[]{:S(2)}) collective-permute-start(f32[3,16384]{1,0:T(4,128)} %fusion.334), channel_id=1, source_target_pairs={{0,2},{1,3},{2,4},{3,5},{4,6},{5,7},{6,8},{7,9},{8,10},{9,11},{10,... | collective-permute-start | bytes 589832 | tf_op jit(solution)/shard_map/ppermute | solution.py:14
  65.9 7.0 %copy-start.50 = (f32[3,16384]{1,0:T(4,128)S(1)}, f32[3,16384]{1,0:T(4,128)}, u32[]{:S(2)}) copy-start(f32[3,16384]{1,0:T(4,128)} %fusion.327) | copy-start | bytes 589828
  65.9 14.0 %copy-start.10 = (f32[512,128]{0,1:T(8,128)S(1)}, f32[512,128]{0,1:T(8,128)}, u32[]{:S(2)}) copy-start(f32[512,128]{0,1:T(8,128)} %copy-done.9) | copy-start | bytes 786436
  70.2 12.7 %collective-permute-start.28 = (f32[3,16384]{1,0:T(4,128)}, f32[3,16384]{1,0:T(4,128)S(1)}, u32[]{:S(2)}, u32[]{:S(2)}) collective-permute-start(f32[3,16384]{1,0:T(4,128)} %fusion.360), channel_id=1, source_target_pairs={{0,31},{1,0},{2,1},{3,2},{4,3},{5,4},{6,5},{7,6},{8,7},{9,8},{10,9... | collective-permute-start | bytes 589832 | tf_op jit(solution)/shard_map/ppermute | solution.py:14
  72.8 12.1 %collective-permute-start.29 = (f32[3,16384]{1,0:T(4,128)}, f32[3,16384]{1,0:T(4,128)S(1)}, u32[]{:S(2)}, u32[]{:S(2)}) collective-permute-start(f32[3,16384]{1,0:T(4,128)} %fusion.349), channel_id=1, source_target_pairs={{0,30},{1,31},{2,0},{3,1},{4,2},{5,3},{6,4},{7,5},{8,6},{9,7},{10,... | collective-permute-start | bytes 589832 | tf_op jit(solution)/shard_map/ppermute | solution.py:14
  72.8 12.1 %collective-permute-start.30 = (f32[3,16384]{1,0:T(4,128)}, f32[3,16384]{1,0:T(4,128)S(1)}, u32[]{:S(2)}, u32[]{:S(2)}) collective-permute-start(f32[3,16384]{1,0:T(4,128)} %fusion.338), channel_id=1, source_target_pairs={{0,1},{1,2},{2,3},{3,4},{4,5},{5,6},{6,7},{7,8},{8,9},{9,10},{10,1... | collective-permute-start | bytes 589832 | tf_op jit(solution)/shard_map/ppermute | solution.py:14
  72.9 24.8 %collective-permute-start.31 = (f32[3,16384]{1,0:T(4,128)S(1)}, f32[3,16384]{1,0:T(4,128)}, u32[]{:S(2)}, u32[]{:S(2)}) collective-permute-start(f32[3,16384]{1,0:T(4,128)S(1)} %copy-done.50), channel_id=1, source_target_pairs={{0,2},{1,3},{2,4},{3,5},{4,6},{5,7},{6,8},{7,9},{8,10},{9,11},{10,... | collective-permute-start | bytes 589832 | tf_op jit(solution)/shard_map/ppermute | solution.py:14
  74.8 39.7 %collective-permute-start.4 = (f32[3,16384]{1,0:T(4,128)}, f32[3,16384]{1,0:T(4,128)}, u32[]{:S(2)}, u32[]{:S(2)}) collective-permute-start(f32[3,16384]{1,0:T(4,128)} %fusion.366), channel_id=1, source_target_pairs={{0,31},{1,0},{2,1},{3,2},{4,3},{5,4},{6,5},{7,6},{8,7},{9,8},{10,9... | collective-permute-start | bytes 589832 | tf_op jit(solution)/shard_map/ppermute | solution.py:14
  82.9 14.7 %copy-start.36 = (f32[3,16384]{1,0:T(4,128)}, f32[3,16384]{1,0:T(4,128)S(1)}, u32[]{:S(2)}) copy-start(f32[3,16384]{1,0:T(4,128)S(1)} %collective-permute-done.28) | copy-start | bytes 589828
  82.9 31.6 %collective-permute-start.5 = (f32[3,16384]{1,0:T(4,128)}, f32[3,16384]{1,0:T(4,128)}, u32[]{:S(2)}, u32[]{:S(2)}) collective-permute-start(f32[3,16384]{1,0:T(4,128)} %fusion.355), channel_id=1, source_target_pairs={{0,30},{1,31},{2,0},{3,1},{4,2},{5,3},{6,4},{7,5},{8,6},{9,7},{10,... | collective-permute-start | bytes 589832 | tf_op jit(solution)/shard_map/ppermute | solution.py:14
  84.9 12.7 %copy-start.39 = (f32[3,16384]{1,0:T(4,128)}, f32[3,16384]{1,0:T(4,128)S(1)}, u32[]{:S(2)}) copy-start(f32[3,16384]{1,0:T(4,128)S(1)} %collective-permute-done.29) | copy-start | bytes 589828
  84.9 29.6 %collective-permute-start.6 = (f32[3,16384]{1,0:T(4,128)}, f32[3,16384]{1,0:T(4,128)}, u32[]{:S(2)}, u32[]{:S(2)}) collective-permute-start(f32[3,16384]{1,0:T(4,128)} %fusion.344), channel_id=1, source_target_pairs={{0,1},{1,2},{2,3},{3,4},{4,5},{5,6},{6,7},{7,8},{8,9},{9,10},{10,1... | collective-permute-start | bytes 589832 | tf_op jit(solution)/shard_map/ppermute | solution.py:14
  84.9 12.7 %copy-start.42 = (f32[3,16384]{1,0:T(4,128)}, f32[3,16384]{1,0:T(4,128)S(1)}, u32[]{:S(2)}) copy-start(f32[3,16384]{1,0:T(4,128)S(1)} %collective-permute-done.30) | copy-start | bytes 589828
  84.9 29.6 %collective-permute-start.7 = (f32[3,16384]{1,0:T(4,128)}, f32[3,16384]{1,0:T(4,128)}, u32[]{:S(2)}, u32[]{:S(2)}) collective-permute-start(f32[3,16384]{1,0:T(4,128)} %fusion.333), channel_id=1, source_target_pairs={{0,2},{1,3},{2,4},{3,5},{4,6},{5,7},{6,8},{7,9},{8,10},{9,11},{10,... | collective-permute-start | bytes 589832 | tf_op jit(solution)/shard_map/ppermute | solution.py:14
  131.2 9.1 %collective-permute-start.33 = (f32[3,16384]{1,0:T(4,128)}, f32[3,16384]{1,0:T(4,128)S(1)}, u32[]{:S(2)}, u32[]{:S(2)}) collective-permute-start(f32[3,16384]{1,0:T(4,128)} %fusion.348), channel_id=1, source_target_pairs={{0,30},{1,31},{2,0},{3,1},{4,2},{5,3},{6,4},{7,5},{8,6},{9,7},{10,... | collective-permute-start | bytes 589832 | tf_op jit(solution)/shard_map/ppermute | solution.py:14
  132.3 9.9 %collective-permute-start.34 = (f32[3,16384]{1,0:T(4,128)S(1)}, f32[3,16384]{1,0:T(4,128)S(1)}, u32[]{:S(2)}, u32[]{:S(2)}) collective-permute-start(f32[3,16384]{1,0:T(4,128)S(1)} %copy-done.52), channel_id=1, source_target_pairs={{0,1},{1,2},{2,3},{3,4},{4,5},{5,6},{6,7},{7,8},{8,9},{9,10},{10,1... | collective-permute-start | bytes 589832 | tf_op jit(solution)/shard_map/ppermute | solution.py:14
  134.0 18.3 %collective-permute-start.35 = (f32[3,16384]{1,0:T(4,128)S(1)}, f32[3,16384]{1,0:T(4,128)S(1)}, u32[]{:S(2)}, u32[]{:S(2)}) collective-permute-start(f32[3,16384]{1,0:T(4,128)S(1)} %copy-done.51), channel_id=1, source_target_pairs={{0,2},{1,3},{2,4},{3,5},{4,6},{5,7},{6,8},{7,9},{8,10},{9,11},{10,... | collective-permute-start | bytes 589832 | tf_op jit(solution)/shard_map/ppermute | solution.py:14
  134.3 23.5 %collective-permute-start.32 = (f32[3,16384]{1,0:T(4,128)S(1)}, f32[3,16384]{1,0:T(4,128)}, u32[]{:S(2)}, u32[]{:S(2)}) collective-permute-start(f32[3,16384]{1,0:T(4,128)S(1)} %fusion.359), channel_id=1, source_target_pairs={{0,31},{1,0},{2,1},{3,2},{4,3},{5,4},{6,5},{7,6},{8,7},{9,8},{10,9... | collective-permute-start | bytes 589832 | tf_op jit(solution)/shard_map/ppermute | solution.py:14
  139.0 33.2 %collective-permute-start.10 = (f32[3,16384]{1,0:T(4,128)}, f32[3,16384]{1,0:T(4,128)}, u32[]{:S(2)}, u32[]{:S(2)}) collective-permute-start(f32[3,16384]{1,0:T(4,128)} %fusion.343), channel_id=1, source_target_pairs={{0,1},{1,2},{2,3},{3,4},{4,5},{5,6},{6,7},{7,8},{8,9},{9,10},{10,1... | collective-permute-start | bytes 589832 | tf_op jit(solution)/shard_map/ppermute | solution.py:14
  140.3 31.9 %collective-permute-start.11 = (f32[3,16384]{1,0:T(4,128)}, f32[3,16384]{1,0:T(4,128)}, u32[]{:S(2)}, u32[]{:S(2)}) collective-permute-start(f32[3,16384]{1,0:T(4,128)} %fusion.332), channel_id=1, source_target_pairs={{0,2},{1,3},{2,4},{3,5},{4,6},{5,7},{6,8},{7,9},{8,10},{9,11},{10,... | collective-permute-start | bytes 589832 | tf_op jit(solution)/shard_map/ppermute | solution.py:14
  142.2 15.6 %copy-start.45 = (f32[3,16384]{1,0:T(4,128)}, f32[3,16384]{1,0:T(4,128)S(1)}, u32[]{:S(2)}) copy-start(f32[3,16384]{1,0:T(4,128)S(1)} %collective-permute-done.34) | copy-start | bytes 589828
  142.2 30.0 %collective-permute-start.9 = (f32[3,16384]{1,0:T(4,128)}, f32[3,16384]{1,0:T(4,128)}, u32[]{:S(2)}, u32[]{:S(2)}) collective-permute-start(f32[3,16384]{1,0:T(4,128)} %fusion.354), channel_id=1, source_target_pairs={{0,30},{1,31},{2,0},{3,1},{4,2},{5,3},{6,4},{7,5},{8,6},{9,7},{10,... | collective-permute-start | bytes 589832 | tf_op jit(solution)/shard_map/ppermute | solution.py:14
  152.3 19.9 %collective-permute-start.8 = (f32[3,16384]{1,0:T(4,128)}, f32[3,16384]{1,0:T(4,128)}, u32[]{:S(2)}, u32[]{:S(2)}) collective-permute-start(f32[3,16384]{1,0:T(4,128)} %fusion.365), channel_id=1, source_target_pairs={{0,31},{1,0},{2,1},{3,2},{4,3},{5,4},{6,5},{7,6},{8,7},{9,8},{10,9... | collective-permute-start | bytes 589832 | tf_op jit(solution)/shard_map/ppermute | solution.py:14
  185.0 10.7 %copy-start.17 = (f32[1,512,128]{1,2,0:T(8,128)S(1)}, f32[1,512,128]{1,2,0:T(8,128)}, u32[]{:S(2)}) copy-start(f32[1,512,128]{1,2,0:T(8,128)} %get-tuple-element.35) | copy-start | bytes 786436
  188.6 14.3 %collective-permute-start.36 = (f32[3,16384]{1,0:T(4,128)}, f32[3,16384]{1,0:T(4,128)S(1)}, u32[]{:S(2)}, u32[]{:S(2)}) collective-permute-start(f32[3,16384]{1,0:T(4,128)} %fusion.358), channel_id=1, source_target_pairs={{0,31},{1,0},{2,1},{3,2},{4,3},{5,4},{6,5},{7,6},{8,7},{9,8},{10,9... | collective-permute-start | bytes 589832 | tf_op jit(solution)/shard_map/ppermute | solution.py:14
  189.3 18.2 %collective-permute-start.37 = (f32[3,16384]{1,0:T(4,128)}, f32[3,16384]{1,0:T(4,128)S(1)}, u32[]{:S(2)}, u32[]{:S(2)}) collective-permute-start(f32[3,16384]{1,0:T(4,128)} %fusion.347), channel_id=1, source_target_pairs={{0,30},{1,31},{2,0},{3,1},{4,2},{5,3},{6,4},{7,5},{8,6},{9,7},{10,... | collective-permute-start | bytes 589832 | tf_op jit(solution)/shard_map/ppermute | solution.py:14
  189.6 17.9 %collective-permute-start.38 = (f32[3,16384]{1,0:T(4,128)}, f32[3,16384]{1,0:T(4,128)S(1)}, u32[]{:S(2)}, u32[]{:S(2)}) collective-permute-start(f32[3,16384]{1,0:T(4,128)} %fusion.336), channel_id=1, source_target_pairs={{0,1},{1,2},{2,3},{3,4},{4,5},{5,6},{6,7},{7,8},{8,9},{9,10},{10,1... | collective-permute-start | bytes 589832 | tf_op jit(solution)/shard_map/ppermute | solution.py:14
  193.1 20.8 %collective-permute-start.39 = (f32[3,16384]{1,0:T(4,128)}, f32[3,16384]{1,0:T(4,128)}, u32[]{:S(2)}, u32[]{:S(2)}) collective-permute-start(f32[3,16384]{1,0:T(4,128)} %fusion.325), channel_id=1, source_target_pairs={{0,2},{1,3},{2,4},{3,5},{4,6},{5,7},{6,8},{7,9},{8,10},{9,11},{10,... | collective-permute-start | bytes 589832 | tf_op jit(solution)/shard_map/ppermute | solution.py:14
  196.7 34.9 %collective-permute-start.12 = (f32[3,16384]{1,0:T(4,128)}, f32[3,16384]{1,0:T(4,128)}, u32[]{:S(2)}, u32[]{:S(2)}) collective-permute-start(f32[3,16384]{1,0:T(4,128)} %fusion.364), channel_id=1, source_target_pairs={{0,31},{1,0},{2,1},{3,2},{4,3},{5,4},{6,5},{7,6},{8,7},{9,8},{10,9... | collective-permute-start | bytes 589832 | tf_op jit(solution)/shard_map/ppermute | solution.py:14
  202.9 11.1 %copy-start.37 = (f32[3,16384]{1,0:T(4,128)}, f32[3,16384]{1,0:T(4,128)S(1)}, u32[]{:S(2)}) copy-start(f32[3,16384]{1,0:T(4,128)S(1)} %collective-permute-done.36) | copy-start | bytes 589828
  202.9 28.7 %collective-permute-start.13 = (f32[3,16384]{1,0:T(4,128)}, f32[3,16384]{1,0:T(4,128)}, u32[]{:S(2)}, u32[]{:S(2)}) collective-permute-start(f32[3,16384]{1,0:T(4,128)} %fusion.353), channel_id=1, source_target_pairs={{0,30},{1,31},{2,0},{3,1},{4,2},{5,3},{6,4},{7,5},{8,6},{9,7},{10,... | collective-permute-start | bytes 589832 | tf_op jit(solution)/shard_map/ppermute | solution.py:14
  207.4 6.5 %copy-start.40 = (f32[3,16384]{1,0:T(4,128)}, f32[3,16384]{1,0:T(4,128)S(1)}, u32[]{:S(2)}) copy-start(f32[3,16384]{1,0:T(4,128)S(1)} %collective-permute-done.37) | copy-start | bytes 589828
  207.4 24.1 %collective-permute-start.14 = (f32[3,16384]{1,0:T(4,128)}, f32[3,16384]{1,0:T(4,128)}, u32[]{:S(2)}, u32[]{:S(2)}) collective-permute-start(f32[3,16384]{1,0:T(4,128)} %fusion.342), channel_id=1, source_target_pairs={{0,1},{1,2},{2,3},{3,4},{4,5},{5,6},{6,7},{7,8},{8,9},{9,10},{10,1... | collective-permute-start | bytes 589832 | tf_op jit(solution)/shard_map/ppermute | solution.py:14
  207.5 6.5 %copy-start.43 = (f32[3,16384]{1,0:T(4,128)}, f32[3,16384]{1,0:T(4,128)S(1)}, u32[]{:S(2)}) copy-start(f32[3,16384]{1,0:T(4,128)S(1)} %collective-permute-done.38) | copy-start | bytes 589828
  207.5 24.1 %collective-permute-start.15 = (f32[3,16384]{1,0:T(4,128)}, f32[3,16384]{1,0:T(4,128)}, u32[]{:S(2)}, u32[]{:S(2)}) collective-permute-start(f32[3,16384]{1,0:T(4,128)} %fusion.331), channel_id=1, source_target_pairs={{0,2},{1,3},{2,4},{3,5},{4,6},{5,7},{6,8},{7,9},{8,10},{9,11},{10,... | collective-permute-start | bytes 589832 | tf_op jit(solution)/shard_map/ppermute | solution.py:14
  243.8 8.4 %copy-start.18 = (f32[1,512,128]{1,2,0:T(8,128)S(1)}, f32[1,512,128]{1,2,0:T(8,128)}, u32[]{:S(2)}) copy-start(f32[1,512,128]{1,2,0:T(8,128)} %get-tuple-element.34) | copy-start | bytes 786436
  247.5 12.9 %collective-permute-start.40 = (f32[3,16384]{1,0:T(4,128)}, f32[3,16384]{1,0:T(4,128)S(1)}, u32[]{:S(2)}, u32[]{:S(2)}) collective-permute-start(f32[3,16384]{1,0:T(4,128)} %fusion.357), channel_id=1, source_target_pairs={{0,31},{1,0},{2,1},{3,2},{4,3},{5,4},{6,5},{7,6},{8,7},{9,8},{10,9... | collective-permute-start | bytes 589832 | tf_op jit(solution)/shard_map/ppermute | solution.py:14
  250.2 12.8 %collective-permute-start.41 = (f32[3,16384]{1,0:T(4,128)}, f32[3,16384]{1,0:T(4,128)S(1)}, u32[]{:S(2)}, u32[]{:S(2)}) collective-permute-start(f32[3,16384]{1,0:T(4,128)} %fusion.346), channel_id=1, source_target_pairs={{0,30},{1,31},{2,0},{3,1},{4,2},{5,3},{6,4},{7,5},{8,6},{9,7},{10,... | collective-permute-start | bytes 589832 | tf_op jit(solution)/shard_map/ppermute | solution.py:14
  250.4 12.6 %collective-permute-start.42 = (f32[3,16384]{1,0:T(4,128)}, f32[3,16384]{1,0:T(4,128)S(1)}, u32[]{:S(2)}, u32[]{:S(2)}) collective-permute-start(f32[3,16384]{1,0:T(4,128)} %fusion.335), channel_id=1, source_target_pairs={{0,1},{1,2},{2,3},{3,4},{4,5},{5,6},{6,7},{7,8},{8,9},{9,10},{10,1... | collective-permute-start | bytes 589832 | tf_op jit(solution)/shard_map/ppermute | solution.py:14
  250.6 26.5 %collective-permute-start.43 = (f32[3,16384]{1,0:T(4,128)}, f32[3,16384]{1,0:T(4,128)}, u32[]{:S(2)}, u32[]{:S(2)}) collective-permute-start(f32[3,16384]{1,0:T(4,128)} %fusion.324), channel_id=1, source_target_pairs={{0,2},{1,3},{2,4},{3,5},{4,6},{5,7},{6,8},{7,9},{8,10},{9,11},{10,... | collective-permute-start | bytes 589832 | tf_op jit(solution)/shard_map/ppermute | solution.py:14
  253.2 37.2 %collective-permute-start.16 = (f32[3,16384]{1,0:T(4,128)}, f32[3,16384]{1,0:T(4,128)}, u32[]{:S(2)}, u32[]{:S(2)}) collective-permute-start(f32[3,16384]{1,0:T(4,128)} %fusion.363), channel_id=1, source_target_pairs={{0,31},{1,0},{2,1},{3,2},{4,3},{5,4},{6,5},{7,6},{8,7},{9,8},{10,9... | collective-permute-start | bytes 589832 | tf_op jit(solution)/shard_map/ppermute | solution.py:14
  260.4 16.7 %copy-start.38 = (f32[3,16384]{1,0:T(4,128)}, f32[3,16384]{1,0:T(4,128)S(1)}, u32[]{:S(2)}) copy-start(f32[3,16384]{1,0:T(4,128)S(1)} %collective-permute-done.40) | copy-start | bytes 589828
  260.4 30.1 %collective-permute-start.17 = (f32[3,16384]{1,0:T(4,128)}, f32[3,16384]{1,0:T(4,128)}, u32[]{:S(2)}, u32[]{:S(2)}) collective-permute-start(f32[3,16384]{1,0:T(4,128)} %fusion.352), channel_id=1, source_target_pairs={{0,30},{1,31},{2,0},{3,1},{4,2},{5,3},{6,4},{7,5},{8,6},{9,7},{10,... | collective-permute-start | bytes 589832 | tf_op jit(solution)/shard_map/ppermute | solution.py:14
  263.0 14.1 %copy-start.41 = (f32[3,16384]{1,0:T(4,128)}, f32[3,16384]{1,0:T(4,128)S(1)}, u32[]{:S(2)}) copy-start(f32[3,16384]{1,0:T(4,128)S(1)} %collective-permute-done.41) | copy-start | bytes 589828
  263.0 27.5 %collective-permute-start.18 = (f32[3,16384]{1,0:T(4,128)}, f32[3,16384]{1,0:T(4,128)}, u32[]{:S(2)}, u32[]{:S(2)}) collective-permute-start(f32[3,16384]{1,0:T(4,128)} %fusion.341), channel_id=1, source_target_pairs={{0,1},{1,2},{2,3},{3,4},{4,5},{5,6},{6,7},{7,8},{8,9},{9,10},{10,1... | collective-permute-start | bytes 589832 | tf_op jit(solution)/shard_map/ppermute | solution.py:14
  263.0 14.1 %copy-start.44 = (f32[3,16384]{1,0:T(4,128)}, f32[3,16384]{1,0:T(4,128)S(1)}, u32[]{:S(2)}) copy-start(f32[3,16384]{1,0:T(4,128)S(1)} %collective-permute-done.42) | copy-start | bytes 589828
  263.0 27.5 %collective-permute-start.19 = (f32[3,16384]{1,0:T(4,128)}, f32[3,16384]{1,0:T(4,128)}, u32[]{:S(2)}, u32[]{:S(2)}) collective-permute-start(f32[3,16384]{1,0:T(4,128)} %fusion.330), channel_id=1, source_target_pairs={{0,2},{1,3},{2,4},{3,5},{4,6},{5,7},{6,8},{7,9},{8,10},{9,11},{10,... | collective-permute-start | bytes 589832 | tf_op jit(solution)/shard_map/ppermute | solution.py:14
  309.1 9.2 %collective-permute-start.20 = (f32[3,16384]{1,0:T(4,128)}, f32[3,16384]{1,0:T(4,128)S(1)}, u32[]{:S(2)}, u32[]{:S(2)}) collective-permute-start(f32[3,16384]{1,0:T(4,128)} %fusion.362), channel_id=1, source_target_pairs={{0,31},{1,0},{2,1},{3,2},{4,3},{5,4},{6,5},{7,6},{8,7},{9,8},{10,9... | collective-permute-start | bytes 589832 | tf_op jit(solution)/shard_map/ppermute | solution.py:14
  311.8 12.3 %collective-permute-start.21 = (f32[3,16384]{1,0:T(4,128)}, f32[3,16384]{1,0:T(4,128)S(1)}, u32[]{:S(2)}, u32[]{:S(2)}) collective-permute-start(f32[3,16384]{1,0:T(4,128)} %fusion.351), channel_id=1, source_target_pairs={{0,30},{1,31},{2,0},{3,1},{4,2},{5,3},{6,4},{7,5},{8,6},{9,7},{10,... | collective-permute-start | bytes 589832 | tf_op jit(solution)/shard_map/ppermute | solution.py:14
  311.8 12.3 %collective-permute-start.22 = (f32[3,16384]{1,0:T(4,128)}, f32[3,16384]{1,0:T(4,128)S(1)}, u32[]{:S(2)}, u32[]{:S(2)}) collective-permute-start(f32[3,16384]{1,0:T(4,128)} %fusion.340), channel_id=1, source_target_pairs={{0,1},{1,2},{2,3},{3,4},{4,5},{5,6},{6,7},{7,8},{8,9},{9,10},{10,1... | collective-permute-start | bytes 589832 | tf_op jit(solution)/shard_map/ppermute | solution.py:14
  312.0 13.5 %collective-permute-start.23 = (f32[3,16384]{1,0:T(4,128)S(1)}, f32[3,16384]{1,0:T(4,128)}, u32[]{:S(2)}, u32[]{:S(2)}) collective-permute-start(f32[3,16384]{1,0:T(4,128)S(1)} %fusion.329), channel_id=1, source_target_pairs={{0,2},{1,3},{2,4},{3,5},{4,6},{5,7},{6,8},{7,9},{8,10},{9,11},{10,... | collective-permute-start | bytes 589832 | tf_op jit(solution)/shard_map/ppermute | solution.py:14
  (35 other events, 72.7 us)
Sparse Core Ops, SparseCore 0:
  358.0 67.1 all-gather.2
